TPU v7x, 128 devices: a whole 4x4x4 slice. The times are simulated.
128 devices in a mesh: cp: 32 (over y, z, core), tp: 4 (over x).
Axes of the slice: x: 4, y: 4, z: 4, core: 2. Of those that a mesh axis runs over, the one named last changes fastest.
Arguments:
- query_rows: bfloat16 [16384, 16384], P(('cp', 'tp')), may hold values from -48 to 48
- token_keys: bfloat16 [16384, 1024], P(('cp', 'tp')), may hold values from -5 to 5
- token_values: bfloat16 [16384, 1024], P(('cp', 'tp')), may hold values from -5 to 5
- doc_lengths: int32 [16], replicated, may hold values from 1 to 2048, 16384 in all
- block_plan: int32 [32, 32], replicated, may hold values from 0 to 31, each once within a row
Outputs:
- attended: bfloat16 [16384, 16384], P(('cp', 'tp'))
Inputs may be any that keep to these rules, and one draw needn't show every extreme that they name: `doc_lengths`: the documents fill all 16384 tokens; one of them holds exactly 2048. Each row of block_plan is a permutation of 0 to 31.
All inputs are finite; a program needn't handle non-finite values.
Results may differ from a plain program's by a relative error of at most 0.012.
Values may be sent and summed in bfloat16 or wider, within the bound.
No kernel may reach another device: no remote copies, remote signals or barrier semaphores. Data moves between devices by JAX's collectives and lax.ppermute only.
A program may use at most 128 MiB of HBM per device.

v0:
```python
import functools
import math
import jax, jax.numpy as jnp, numpy as np
from jax import lax
from jax.experimental import pallas as pl
from jax.experimental.pallas import tpu as pltpu
from jax.sharding import PartitionSpec as P

HD = 128
BLOCK = 512
REACH = 2048
PAD = 128
TILE = 128
KEYS = 256
BIG = float(2 ** 20)
NDOC = 16
SEQ = 16384


def scaled_frequencies(head_width):
    exponents = np.arange(0, head_width, 2) / head_width
    inverse = 1.0 / np.power(500000.0, exponents)
    wavelength = 2.0 * np.pi / inverse
    smooth = (8192.0 / wavelength - 1.0) / 3.0
    blended = (1.0 - smooth) * inverse / 8.0 + smooth * inverse
    middle = np.where(wavelength > 8192.0, inverse / 8.0, blended)
    return np.where(wavelength < 2048.0, inverse, middle)


def rotation_tables():
    f = scaled_frequencies(HD)
    coarse = np.arange(SEQ // 128)[:, None] * 128.0 * f[None, :]
    fine = np.arange(128)[:, None] * 1.0 * f[None, :]
    parts = (np.cos(coarse), np.sin(coarse), np.cos(fine), np.sin(fine))
    return np.concatenate([np.concatenate([p, p], axis=1) for p in parts], axis=0).astype(np.float32)


def attn_kernel(heads, doc_ref, plan_ref, at_ref, tab_ref, q_ref, k4, k3, k2, k1, k0, out_ref, kaug, vt, qs, inv):
    s = pl.program_id(0) * 8 + at_ref[0]
    lane = lax.broadcasted_iota(jnp.int32, (1, 128), 1)
    first_token = s * BLOCK
    starts = jnp.zeros((1, 128), jnp.int32)
    ends = jnp.zeros((1, 128), jnp.int32)
    bounds = []
    begin = jnp.int32(0)
    for d in range(NDOC):
        bounds.append(begin)
        end = begin + doc_ref[d]
        starts = jnp.where(lane == d, begin, starts)
        ends = jnp.where(lane == d, end, ends)
        begin = end
    starts = jnp.where(lane == NDOC, -(1 << 20), starts)

    def note(r, c):
        inv[plan_ref[s, r]] = r
        return c

    lax.fori_loop(0, 32, note, 0)
    sign = jnp.where(lane < 64, -1.0, 1.0)

    def tables(pos):
        u = jnp.maximum(pos, 0) // 128
        C = tab_ref[pl.ds(u, 1), :]
        S = tab_ref[pl.ds(u + 128, 1), :]
        c = tab_ref[pl.ds(256, 128), :]
        n = tab_ref[pl.ds(384, 128), :]
        return C * c - S * n, (S * c + C * n) * sign

    def inside(pos):
        p = pos + lax.broadcasted_iota(jnp.int32, (128, 128), 0)
        return (p >= starts) & (p < ends)

    def rotated(x, cos, sin):
        x = x.astype(jnp.float32)
        return (x * cos + pltpu.roll(x, 64, 1) * sin).astype(jnp.bfloat16)

    base = first_token - REACH
    kaug[0:PAD, 0:128] = jnp.zeros((PAD, 128), jnp.bfloat16)
    kaug[0:PAD, 128:256] = jnp.where(inside(base - PAD), 1.0, 0.0).astype(jnp.bfloat16)
    vt[:, 0:PAD] = jnp.zeros((128, PAD), jnp.bfloat16)
    for b, ref in enumerate((k4, k3, k2, k1, k0)):
        for i in range(4):
            pos = base + b * BLOCK + i * 128
            at = PAD + b * BLOCK + i * 128
            cos, sin = tables(pos)
            kaug[at:at + 128, 0:128] = rotated(ref[0, 0, i, :, 0:128], cos, sin)
            kaug[at:at + 128, 128:256] = jnp.where(inside(pos), 1.0, 0.0).astype(jnp.bfloat16)
            vt[:, at:at + 128] = ref[0, 0, i, :, 128:256].T

    scale = math.log2(math.e) / math.sqrt(HD)

    def tile(t, carry):
        pos = first_token + t * TILE
        cos, sin = tables(pos)
        bias = jnp.where(inside(pos), 0.0, -BIG).astype(jnp.bfloat16)
        for h in range(heads):
            qs[h * 128:h * 128 + 128, 0:128] = rotated(q_ref[0, t, :, h * 128:h * 128 + 128], cos, sin)
            qs[h * 128:h * 128 + 128, 128:256] = bias
        low = jnp.int32(0)
        for d in range(NDOC):
            low = jnp.where(bounds[d] <= pos, bounds[d], low)
        count = (pos + TILE - low + KEYS - 1) // KEYS
        end = PAD + REACH + TILE + t * TILE

        def score(hp, k):
            at = pl.multiple_of(end - KEYS * (k + 1), 128)
            sc = lax.dot_general(kaug[pl.ds(at, KEYS), :], qs[hp * 256:hp * 256 + 256, :],
                                 (((1,), (1,)), ((), ())), preferred_element_type=jnp.float32)
            if k == 0:
                key = lax.broadcasted_iota(jnp.int32, (KEYS, 256), 0) - (KEYS - 128)
                tok = lax.broadcasted_iota(jnp.int32, (KEYS, 256), 1) & 127
                sc = jnp.where(key <= tok, sc, -1e30)
            return sc

        def mix(sc, high, k):
            at = pl.multiple_of(end - KEYS * (k + 1), 128)
            raised = jnp.exp2((sc - high) * scale)
            part = jnp.sum(raised, axis=0, keepdims=True)
            mixed = lax.dot_general(vt[:, pl.ds(at, KEYS)], raised.astype(jnp.bfloat16),
                                    (((1,), (0,)), ((), ())), preferred_element_type=jnp.float32)
            return part, mixed

        def finish(hp, acc, total):
            o = (acc / total).T.astype(jnp.bfloat16)
            for a in range(2):
                col = hp * 256 + a * 128
                for p in range(8):
                    out_ref[inv[t * 8 + p], 0, :, col:col + 128] = o[a * 128 + p * 16:a * 128 + p * 16 + 16]

        def run(n):
            pairs = range(heads // 2)
            scores = [[score(hp, k) for k in range(n)] for hp in pairs]
            sums = []
            for hp in pairs:
                tops = [jnp.max(sc, axis=0, keepdims=True) for sc in scores[hp]]
                high = functools.reduce(jnp.maximum, tops)
                got = [mix(scores[hp][k], high, k) for k in range(n)]
                sums.append([functools.reduce(jnp.add, list(g)) for g in zip(*got)])
            for hp in pairs:
                finish(hp, sums[hp][1], sums[hp][0])

        for n in range(1, 10):
            pl.when(count == n)(functools.partial(run, n))
        return carry

    lax.fori_loop(0, BLOCK // TILE, tile, 0)


def attend(heads, docs, plan, at, tab, q, kv):
    smem = pl.BlockSpec(memory_space=pltpu.SMEM)

    def back(d):
        def index(y, docs_ref, plan_ref, at_ref):
            b = jnp.maximum(y * 8 + at_ref[0] - d, 0)
            return (b % 8, b // 8, 0, 0, 0)

        return pl.BlockSpec((1, 1, 4, 128, 256), index)

    return pl.pallas_call(
        lambda *r: attn_kernel(heads, *r),
        out_shape=jax.ShapeDtypeStruct((32, 4, 16, heads * 128), jnp.bfloat16),
        grid_spec=pltpu.PrefetchScalarGridSpec(
            num_scalar_prefetch=3,
            grid=(4,),
            in_specs=[
                pl.BlockSpec((512, 128), lambda y, *_: (0, 0)),
                pl.BlockSpec((1, 4, 128, heads * 128), lambda y, *_: (y, 0, 0, 0)),
            ] + [back(d) for d in (4, 3, 2, 1, 0)],
            out_specs=pl.BlockSpec((32, 1, 16, heads * 128), lambda y, *_: (0, y, 0, 0)),
            scratch_shapes=[
                pltpu.VMEM((PAD + REACH + BLOCK, 256), jnp.bfloat16),
                pltpu.VMEM((128, PAD + REACH + BLOCK), jnp.bfloat16),
                pltpu.VMEM((heads * 128, 256), jnp.bfloat16),
                pltpu.SMEM((32,), jnp.int32),
            ],
        ),
        compiler_params=pltpu.CompilerParams(vmem_limit_bytes=48 << 20),
        name="attend",
    )(docs, plan, at, tab, q, kv, kv, kv, kv, kv)


AXES = ("y", "z", "core", "x")
CHUNKS = 2


def split_kernel(rows, *outs):
    width = 1024 // len(outs)
    for g in range(4):
        for j, out in enumerate(outs):
            out[g] = rows[:, g * 1024 + j * width:g * 1024 + (j + 1) * width]


def split(rows):
    width = 1024 // CHUNKS
    return pl.pallas_call(
        split_kernel,
        grid=(4,),
        out_shape=[jax.ShapeDtypeStruct((16, 128, width), jnp.bfloat16)] * CHUNKS,
        in_specs=[pl.BlockSpec((128, 4096), lambda g: (0, g))],
        out_specs=[pl.BlockSpec((4, 128, width), lambda g: (g, 0, 0))] * CHUNKS,
        name="split",
    )(rows)


def place_kernel(*refs):
    out = refs[-1]
    width = 1024 // CHUNKS
    for j, part in enumerate(refs[:-1]):
        for b in range(8):
            for x in range(4):
                out[b * 16:b * 16 + 16, x * 1024 + j * width:x * 1024 + (j + 1) * width] = part[0, b, x]


def place(parts):
    width = 1024 // CHUNKS
    return pl.pallas_call(
        place_kernel,
        grid=(4,),
        out_shape=jax.ShapeDtypeStruct((128, 16384), jnp.bfloat16),
        in_specs=[pl.BlockSpec((1, 8, 4, 16, width), lambda y: (y, 0, 0, 0, 0))] * CHUNKS,
        out_specs=pl.BlockSpec((128, 4096), lambda y: (0, y)),
        name="place",
    )(*parts)


def on_device(query_rows, token_keys, token_values, doc_lengths, block_plan):
    at = (lax.axis_index("z") * 2 + lax.axis_index("core")).astype(jnp.int32).reshape(1)
    kv = jnp.concatenate([token_keys.reshape(128, 8, 128), token_values.reshape(128, 8, 128)], axis=2)
    kv = jnp.repeat(kv.transpose(1, 0, 2), 2, axis=0)
    kv = lax.all_to_all(kv, ("y", "x"), split_axis=0, concat_axis=0, tiled=True)
    kv = lax.all_gather(kv.reshape(4, 4, 128, 256), ("z", "core"), axis=0)
    tab = jnp.asarray(rotation_tables())
    width = 1024 // CHUNKS
    done = []
    for part in split(query_rows):
        part = lax.all_to_all(part, ("y", "x"), split_axis=0, concat_axis=0, tiled=True)
        o = attend(8 // CHUNKS, doc_lengths, block_plan, at, tab, part.reshape(4, 4, 128, width), kv)
        o = lax.all_to_all(o.reshape(128, 16, width), AXES, split_axis=0, concat_axis=0, tiled=True)
        done.append(o.reshape(4, 8, 4, 16, width))
    return place(done)


def solution(mesh):
    fine = jax.sharding.Mesh(mesh.devices.reshape(4, 4, 2, 4), AXES)
    rows = P(AXES, None)
    return jax.shard_map(
        on_device, mesh=fine, in_specs=(rows, rows, rows, P(), P()), out_specs=rows, check_vma=False
    )
```

profile of v0, /device:TPU:1, one launch (start us, length us, event | category | flops | bytes accessed | tf_op | source)
XLA Modules:
  0.0 207.3 jit_solution(10782255061961520933)
XLA Ops:
  6.5 0.0 all-gather.2.cloned.1.call-start
  6.5 1.0 copy.9
  7.5 1.0 copy.10
  8.5 0.1 maximum_bitcast_fusion
  8.6 0.1 copy.8
  8.7 0.1 broadcast_in_dim.3
  8.8 23.5 %all_to_all.25 = bf16[16,128,256]{2,1,0:T(8,128)(2,1)} all-to-all(bf16[16,128,256]{2,1,0:T(8,128)(2,1)S(1)} %bitcast.21), channel_id=1, replica_groups=mesh['y'=4,'z'=4,'core'=2,'x'=4] {'y','x'}, dimensions={0} | all-to-all | bytes 2097152 | tf_op jit(solution)/shard_map/all_to_all | solution.py:230
  32.3 0.0 all-gather.2.cloned.1.call-update
  32.4 4.7 %split.1 = (bf16[16,128,512]{2,1,0:T(8,128)(2,1)}, bf16[16,128,512]{2,1,0:T(8,128)(2,1)}) custom-call(bf16[128,16384]{1,0:T(8,128)(2,1)} %rows.1), custom_call_target="tpu_custom_call" | custom-call | tf_op jit(solution)/shard_map/split/pallas_call | solution.py:195
  37.1 31.4 %all_to_all.26 = bf16[16,128,512]{2,1,0:T(8,128)(2,1)} all-to-all(bf16[16,128,512]{2,1,0:T(8,128)(2,1)} %get-tuple-element.7), channel_id=1, replica_groups=mesh['y'=4,'z'=4,'core'=2,'x'=4] {'y','x'}, dimensions={0} | all-to-all | bytes 4194304 | tf_op jit(solution)/shard_map/all_to_all | solution.py:236
  68.5 3.9 %all-to-all-start.3 = ((bf16[16,128,512]{2,1,0:T(8,128)(2,1)}), bf16[16,128,512]{2,1,0:T(8,128)(2,1)S(1)}, u32[]{:S(2)}, u32[]{:S(2)}) async-start(bf16[16,128,512]{2,1,0:T(8,128)(2,1)} %get-tuple-element.8), calls=%async_computation.3 | async-start | bytes 4194304 | tf_op jit(solution)/shard_map/all_to_all | solution.py:236
  72.4 10.3 %all-gather.2.cloned.1.call-done.r_5_.r_6_.r_7_.r_8_.r_9_ = bf16[8,4,4,128,256]{4,3,2,1,0:T(8,128)(2,1)} async-done(((bf16[1,4,4,128,256]{4,3,2,1,0:T(8,128)(2,1)}), bf16[8,4,4,128,256]{4,3,2,1,0:T(8,128)(2,1)}) %all-gather.2.cloned.1.call-update) | async-done | bytes 8388624 | tf_op jit(solution)/shard_map/all_gather | solution.py:231
  82.7 1.6 copy-done
  84.3 24.2 %attend.2 = bf16[32,4,16,512]{3,2,1,0:T(8,128)(2,1)S(1)} custom-call(s32[16]{0:T(128)S(1)} %copy-done.5, s32[32,32]{1,0:T(8,128)S(1)} %copy-done.4, s32[1]{0:T(128)} %bitcast.r_2_, f32[512,128]{1,0:T(8,128)S(1)} %copy-done.3, bf16[4,4,128,512]{3,2,1,0:T(8,128)(2,1)S(1)} %bitcast.16, ...), custom_call_target="tpu_custom_call" | custom-call | tf_op jit(solution)/shard_map/attend/pallas_call | solution.py:159
  108.5 0.0 copy-start.1
  108.5 1.3 copy-done.1
  109.8 0.0 all-to-all-done.3
  109.8 14.2 %all-to-all-start.2 = ((bf16[128,16,512]{2,1,0:T(8,128)(2,1)}), bf16[128,16,512]{2,1,0:T(8,128)(2,1)}, u32[]{:S(2)}, u32[]{:S(2)}) async-start(bf16[128,16,512]{2,1,0:T(8,128)(2,1)} %bitcast.17), calls=%async_computation.2 | async-start | bytes 4194304 | tf_op jit(solution)/shard_map/all_to_all | solution.py:238
  124.1 24.2 %attend.3 = bf16[32,4,16,512]{3,2,1,0:T(8,128)(2,1)S(1)} custom-call(s32[16]{0:T(128)S(1)} %copy-done.5, s32[32,32]{1,0:T(8,128)S(1)} %copy-done.4, s32[1]{0:T(128)} %bitcast.r_2_, f32[512,128]{1,0:T(8,128)S(1)} %copy-done.3, bf16[4,4,128,512]{3,2,1,0:T(8,128)(2,1)S(1)} %bitcast.15, ...), custom_call_target="tpu_custom_call" | custom-call | tf_op jit(solution)/shard_map/attend/pallas_call | solution.py:159
  148.3 0.0 copy-start.2
  148.3 1.3 copy-done.2
  149.6 5.1 %all-to-all-done.2 = bf16[128,16,512]{2,1,0:T(8,128)(2,1)} async-done(((bf16[128,16,512]{2,1,0:T(8,128)(2,1)}), bf16[128,16,512]{2,1,0:T(8,128)(2,1)}, u32[]{:S(2)}, u32[]{:S(2)}) %all-to-all-start.2) | async-done | bytes 2097184 | tf_op jit(solution)/shard_map/all_to_all | solution.py:238
  154.7 41.1 %all_to_all.27 = bf16[128,16,512]{2,1,0:T(8,128)(2,1)} all-to-all(bf16[128,16,512]{2,1,0:T(8,128)(2,1)} %bitcast.18), channel_id=1, replica_groups=mesh['y'=4,'z'=4,'core'=2,'x'=4] {'y','z','core','x'}, dimensions={0} | all-to-all | bytes 4194304 | tf_op jit(solution)/shard_map/all_to_all | solution.py:238
  195.7 4.7 %place.1 = bf16[128,16384]{1,0:T(8,128)(2,1)} custom-call(bf16[4,8,4,16,512]{4,3,2,1,0:T(8,128)(2,1)} %bitcast.6.refs_0_, bf16[4,8,4,16,512]{4,3,2,1,0:T(8,128)(2,1)} %bitcast.19), custom_call_target="tpu_custom_call" | custom-call | tf_op jit(solution)/shard_map/place/pallas_call | solution.py:216
  (7 shorter events, 0.0 us)
Async XLA Ops:
  6.5 76.2 %all-gather.2.cloned.1.call-start = ((), (), s32[]{:S(2)}) async-start(), calls=%async_computation.5 | async-start | bytes 9437184 | tf_op jit(solution)/shard_map/all_gather | solution.py:231
  68.5 14.2 %copy-start.3 = (f32[512,128]{1,0:T(8,128)S(1)}, f32[512,128]{1,0:T(8,128)}, u32[]{:S(2)}) copy-start(f32[512,128]{1,0:T(8,128)} %constant.14.clone.r_3_) | copy-start | bytes 786436
  68.5 14.2 %copy-start.4 = (s32[32,32]{1,0:T(8,128)S(1)}, s32[32,32]{1,0:T(8,128)}, u32[]{:S(2)}) copy-start(s32[32,32]{1,0:T(8,128)} %r_1_.3) | copy-start | bytes 12292
  68.5 14.2 %copy-start.5 = (s32[16]{0:T(128)S(1)}, s32[16]{0:T(128)}, u32[]{:S(2)}) copy-start(s32[16]{0:T(128)} %r_0_.3) | copy-start | bytes 196
  68.5 41.3 %all-to-all-start.3 = ((bf16[16,128,512]{2,1,0:T(8,128)(2,1)}), bf16[16,128,512]{2,1,0:T(8,128)(2,1)S(1)}, u32[]{:S(2)}, u32[]{:S(2)}) async-start(bf16[16,128,512]{2,1,0:T(8,128)(2,1)} %get-tuple-element.8), calls=%async_computation.3 | async-start | bytes 4194304 | tf_op jit(solution)/shard_map/all_to_all | solution.py:236
  82.7 1.6 copy-start
  108.5 1.3 copy-start.1
  109.8 44.9 %all-to-all-start.2 = ((bf16[128,16,512]{2,1,0:T(8,128)(2,1)}), bf16[128,16,512]{2,1,0:T(8,128)(2,1)}, u32[]{:S(2)}, u32[]{:S(2)}) async-start(bf16[128,16,512]{2,1,0:T(8,128)(2,1)} %bitcast.17), calls=%async_computation.2 | async-start | bytes 4194304 | tf_op jit(solution)/shard_map/all_to_all | solution.py:238
  148.3 1.3 copy-start.2
Sparse Core Ops, SparseCore 0:
  32.5 50.1 all-gather.1
where the time goes:
time: 207 us
  blocking collectives  96 us (46%)
  Pallas kernels  57.9 us (28%)
  starting transfers between devices  18.1 us (9%)
  waiting for transfers between devices  15.4 us (7%)
  between operations  13.5 us (7%)
  local copies, waits for them, and re-layouts  6.4 us (3%)
    pallas_call x2, Pallas kernels, attend(): pl.pallas_call(lambda *r: attn_kernel(heads, *r), out_shape=jax.ShapeDtyp...  48.4 us
    all_to_all x1, blocking collectives, on_device(): lax.all_to_all(o.reshape(128, 16, width), AXES, split_axis=0, concat_axis...  41.1 us
    all_to_all x1, blocking collectives, on_device(): lax.all_to_all(part, ('y', 'x'), split_axis=0, concat_axis=0, tiled=True)  31.4 us
    all_to_all x1, blocking collectives, on_device(): kv = lax.all_to_all(kv, ('y', 'x'), split_axis=0, concat_axis=0, tiled=True)  23.5 us
    all_to_all x1, starting transfers between devices, on_device(): lax.all_to_all(o.reshape(128, 16, width), AXES, split_axis=0, concat_axis...  14.2 us
    all_gather x1, waiting for transfers between devices, on_device(): kv = lax.all_gather(kv.reshape(4, 4, 128, 256), ('z', 'core'), axis=0)  10.3 us
    unnamed x14, local copies, waits for them, and re-layouts  6.2 us
    all_to_all x1, waiting for transfers between devices, on_device(): lax.all_to_all(o.reshape(128, 16, width), AXES, split_axis=0, concat_axis...  5.06 us
  transfers between devices with their start and end apart: 3, of which 2 were waited for; matrix products, arithmetic and copies ran while one was open for 0% of the time, Pallas kernels for 26%

commit v1 on v0

--- a/solution.py
+++ b/solution.py
@@ -35,7 +35,7 @@
     return np.concatenate([np.concatenate([p, p], axis=1) for p in parts], axis=0).astype(np.float32)
 
 
-def attn_kernel(heads, doc_ref, plan_ref, at_ref, tab_ref, q_ref, k4, k3, k2, k1, k0, out_ref, kaug, vt, qs, inv):
+def attn_kernel(heads, doc_ref, plan_ref, at_ref, tab_ref, q_ref, k4, v4, k3, k2, k1, k0, out_ref, kaug, vt, qs, inv):
     s = pl.program_id(0) * 8 + at_ref[0]
     lane = lax.broadcasted_iota(jnp.int32, (1, 128), 1)
     first_token = s * BLOCK
@@ -78,14 +78,15 @@
     kaug[0:PAD, 0:128] = jnp.zeros((PAD, 128), jnp.bfloat16)
     kaug[0:PAD, 128:256] = jnp.where(inside(base - PAD), 1.0, 0.0).astype(jnp.bfloat16)
     vt[:, 0:PAD] = jnp.zeros((128, PAD), jnp.bfloat16)
-    for b, ref in enumerate((k4, k3, k2, k1, k0)):
+    for b, (kr, vr, vc) in enumerate(
+            ((k4, v4, 0), (k3, k3, 128), (k2, k2, 128), (k1, k1, 128), (k0, k0, 128))):
         for i in range(4):
             pos = base + b * BLOCK + i * 128
             at = PAD + b * BLOCK + i * 128
             cos, sin = tables(pos)
-            kaug[at:at + 128, 0:128] = rotated(ref[0, 0, i, :, 0:128], cos, sin)
+            kaug[at:at + 128, 0:128] = rotated(kr[0, i, :, 0:128], cos, sin)
             kaug[at:at + 128, 128:256] = jnp.where(inside(pos), 1.0, 0.0).astype(jnp.bfloat16)
-            vt[:, at:at + 128] = ref[0, 0, i, :, 128:256].T
+            vt[:, at:at + 128] = vr[0, i, :, vc:vc + 128].T
 
     scale = math.log2(math.e) / math.sqrt(HD)
 
@@ -149,13 +150,13 @@
 def attend(heads, docs, plan, at, tab, q, kv):
     smem = pl.BlockSpec(memory_space=pltpu.SMEM)
 
-    def back(d):
+    def back(d, width):
         def index(y, docs_ref, plan_ref, at_ref):
-            b = jnp.maximum(y * 8 + at_ref[0] - d, 0)
-            return (b % 8, b // 8, 0, 0, 0)
-
-        return pl.BlockSpec((1, 1, 4, 128, 256), index)
-
+            return (jnp.maximum(jnp.where(at_ref[0] < d, y - 1, y), 0), 0, 0, 0)
+
+        return pl.BlockSpec((1, 4, 128, width), index)
+
+    work = 16 * heads * 128 * 9 * 256 * 2 * 512
     return pl.pallas_call(
         lambda *r: attn_kernel(heads, *r),
         out_shape=jax.ShapeDtypeStruct((32, 4, 16, heads * 128), jnp.bfloat16),
@@ -165,7 +166,7 @@
             in_specs=[
                 pl.BlockSpec((512, 128), lambda y, *_: (0, 0)),
                 pl.BlockSpec((1, 4, 128, heads * 128), lambda y, *_: (y, 0, 0, 0)),
-            ] + [back(d) for d in (4, 3, 2, 1, 0)],
+            ] + [back(4, 128), back(4, 128), back(3, 256), back(2, 256), back(1, 256), back(0, 256)],
             out_specs=pl.BlockSpec((32, 1, 16, heads * 128), lambda y, *_: (0, y, 0, 0)),
             scratch_shapes=[
                 pltpu.VMEM((PAD + REACH + BLOCK, 256), jnp.bfloat16),
@@ -175,12 +176,28 @@
             ],
         ),
         compiler_params=pltpu.CompilerParams(vmem_limit_bytes=48 << 20),
+        cost_estimate=pl.CostEstimate(flops=work, bytes_accessed=16 << 20, transcendentals=0),
         name="attend",
-    )(docs, plan, at, tab, q, kv, kv, kv, kv, kv)
+    )(docs, plan, at, tab, q, *kv)
 
 
 AXES = ("y", "z", "core", "x")
 CHUNKS = 2
+
+
+def pack_kernel(keys, values, out):
+    for g in range(8):
+        for twin in range(2):
+            out[2 * g + twin, :, 0:128] = keys[:, g * 128:g * 128 + 128]
+            out[2 * g + twin, :, 128:256] = values[:, g * 128:g * 128 + 128]
+
+
+def pack(keys, values):
+    return pl.pallas_call(
+        pack_kernel,
+        out_shape=jax.ShapeDtypeStruct((16, 128, 256), jnp.bfloat16),
+        name="pack",
+    )(keys, values)
 
 
 def split_kernel(rows, *outs):
@@ -198,6 +215,7 @@
         out_shape=[jax.ShapeDtypeStruct((16, 128, width), jnp.bfloat16)] * CHUNKS,
         in_specs=[pl.BlockSpec((128, 4096), lambda g: (0, g))],
         out_specs=[pl.BlockSpec((4, 128, width), lambda g: (g, 0, 0))] * CHUNKS,
+        cost_estimate=pl.CostEstimate(flops=2 << 30, bytes_accessed=8 << 20, transcendentals=0),
         name="split",
     )(rows)
 
@@ -223,16 +241,32 @@
     )(*parts)
 
 
+def ring(a, by):
+    return lax.ppermute(a, "z", [(i, (i + by) % 4) for i in range(4)])
+
+
+def swap(a):
+    return lax.ppermute(a, "core", [(0, 1), (1, 0)])
+
+
 def on_device(query_rows, token_keys, token_values, doc_lengths, block_plan):
     at = (lax.axis_index("z") * 2 + lax.axis_index("core")).astype(jnp.int32).reshape(1)
-    kv = jnp.concatenate([token_keys.reshape(128, 8, 128), token_values.reshape(128, 8, 128)], axis=2)
-    kv = jnp.repeat(kv.transpose(1, 0, 2), 2, axis=0)
-    kv = lax.all_to_all(kv, ("y", "x"), split_axis=0, concat_axis=0, tiled=True)
-    kv = lax.all_gather(kv.reshape(4, 4, 128, 256), ("z", "core"), axis=0)
+    core = lax.axis_index("core")
+    kv = pack(token_keys, token_values)
+    own = lax.all_to_all(kv, ("y", "x"), split_axis=0, concat_axis=0, tiled=True).reshape(4, 4, 128, 256)
+    parts = split(query_rows)
+    own, *parts = lax.optimization_barrier((own, *parts))
+    near = ring(own, 1)
+    left_values = ring(own[..., 128:], -1)
+    far_keys = ring(near[..., :128], 1)
+    far_values = ring(left_values, -1)
+    first = swap(jnp.where(core == 0, own, near))
+    third = swap(jnp.where(core == 0, near, jnp.concatenate([far_keys, far_values], axis=-1)))
+    kv = (far_keys, far_values, third, near, first, own)
     tab = jnp.asarray(rotation_tables())
     width = 1024 // CHUNKS
     done = []
-    for part in split(query_rows):
+    for part in parts:
         part = lax.all_to_all(part, ("y", "x"), split_axis=0, concat_axis=0, tiled=True)
         o = attend(8 // CHUNKS, doc_lengths, block_plan, at, tab, part.reshape(4, 4, 128, width), kv)
         o = lax.all_to_all(o.reshape(128, 16, width), AXES, split_axis=0, concat_axis=0, tiled=True)

time: 207 us -> 189 us (0.913)
  blocking collectives: 96 us -> 38.6 us
  waiting for transfers between devices: 15.4 us -> 44.6 us
  starting transfers between devices: 18.1 us -> 35 us
  between operations: 13.5 us -> 0.1 us
  Pallas kernels: 57.9 us -> 66.5 us
  local copies, waits for them, and re-layouts: 6.4 us -> 1.01 us
    all_to_all x2 -> x0, blocking collectives: 54.9 us -> none  [the longest x1 31.4 us: on_device(): lax.all_to_all(part, ('y', 'x'), split_axis=0, concat_axis=0, tiled=True)]
    ppermute x0 -> x6, waiting for transfers between devices: none -> 25 us  [the longest x4 25 us: ring(): return lax.ppermute(a, 'z', [(i, (i + by) % 4) for i in range(4)])]
    all_to_all x0 -> x1, waiting for transfers between devices: none -> 11.3 us  [on_device(): lax.all_to_all(kv, ('y', 'x'), split_axis=0, concat_axis=0, tiled=True)]
    ppermute x0 -> x6, starting transfers between devices: none -> 11.1 us  [the longest x4 7.09 us: ring(): return lax.ppermute(a, 'z', [(i, (i + by) % 4) for i in range(4)])]
    all_gather x1 -> x0, waiting for transfers between devices: 10.3 us -> none  [on_device(): kv = lax.all_gather(kv.reshape(4, 4, 128, 256), ('z', 'core'), axis=0)]
    all_to_all x1, starting transfers between devices: 14.2 us -> 5.9 us  [on_device(): lax.all_to_all(o.reshape(128, 16, width), AXES, split_axis=0, concat_axis...]
    all_to_all x0 -> x1, starting transfers between devices: none -> 7.57 us  [on_device(): lax.all_to_all(kv, ('y', 'x'), split_axis=0, concat_axis=0, tiled=True)]
    all_to_all x1 -> x2, starting transfers between devices: 3.85 us -> 10.5 us  [on_device(): lax.all_to_all(part, ('y', 'x'), split_axis=0, concat_axis=0, tiled=True)]
  transfers between devices with their start and end apart: 3 -> 10, of which waited for: 2 -> 6; matrix products, arithmetic and copies ran while one was open for 0% -> 2% of each run, Pallas kernels for 26% -> 32%
where the time goes in v1:
time: 189 us; the launch traced here: 188 us
  Pallas kernels  66.5 us (35%)
  waiting for transfers between devices  44.6 us (24%)
  blocking collectives  38.6 us (20%)
  starting transfers between devices  35 us (19%)
  other arithmetic  1.97 us (1%)
    pallas_call x2, Pallas kernels, attend(): pl.pallas_call(lambda *r: attn_kernel(heads, *r), out_shape=jax.ShapeDtyp...  54.9 us
    all_to_all x1, blocking collectives, on_device(): lax.all_to_all(o.reshape(128, 16, width), AXES, split_axis=0, concat_axis...  38.6 us
    ppermute x4, waiting for transfers between devices, ring(): return lax.ppermute(a, 'z', [(i, (i + by) % 4) for i in range(4)])  25 us
    all_to_all x1, waiting for transfers between devices, on_device(): lax.all_to_all(kv, ('y', 'x'), split_axis=0, concat_axis=0, tiled=True)  11.3 us
    all_to_all x2, starting transfers between devices, on_device(): lax.all_to_all(part, ('y', 'x'), split_axis=0, concat_axis=0, tiled=True)  10.5 us
    all_to_all x1, starting transfers between devices, on_device(): lax.all_to_all(kv, ('y', 'x'), split_axis=0, concat_axis=0, tiled=True)  7.57 us
    ppermute x4, starting transfers between devices, ring(): return lax.ppermute(a, 'z', [(i, (i + by) % 4) for i in range(4)])  7.09 us
    all_to_all x1, starting transfers between devices, on_device(): lax.all_to_all(o.reshape(128, 16, width), AXES, split_axis=0, concat_axis...  5.9 us
  transfers between devices with their start and end apart: 10, of which 6 were waited for; matrix products, arithmetic and copies ran while one was open for 2% of the time, Pallas kernels for 32%

profile of v1, /device:TPU:1, one launch (start us, length us, event | category | flops | bytes accessed | tf_op | source)
XLA Modules:
  0.0 187.9 jit_solution(15956218881066133817)
XLA Ops:
  0.0 2.1 %pack.1 = bf16[16,128,256]{2,1,0:T(8,128)(2,1)} custom-call(bf16[128,1024]{1,0:T(8,128)(2,1)} %keys.1, bf16[128,1024]{1,0:T(8,128)(2,1)} %values.1), custom_call_target="tpu_custom_call" | custom-call | tf_op jit(solution)/shard_map/pack/pallas_call | solution.py:196
  2.1 7.6 %all-to-all-start = ((bf16[16,128,256]{2,1,0:T(8,128)(2,1)}), bf16[16,128,256]{2,1,0:T(8,128)(2,1)S(1)}, u32[]{:S(2)}, u32[]{:S(2)}) async-start(bf16[16,128,256]{2,1,0:T(8,128)(2,1)} %pack.1), calls=%async_computation | async-start | bytes 2097152 | tf_op jit(solution)/shard_map/all_to_all | solution.py:256
  9.7 4.7 %split.1 = (bf16[16,128,512]{2,1,0:T(8,128)(2,1)}, bf16[16,128,512]{2,1,0:T(8,128)(2,1)}) custom-call(bf16[128,16384]{1,0:T(8,128)(2,1)} %rows.1), custom_call_target="tpu_custom_call" | custom-call | flops 2147483648 | bytes 8388608 | tf_op jit(solution)/shard_map/split/pallas_call | solution.py:212
  14.5 11.3 %all-to-all-done = bf16[16,128,256]{2,1,0:T(8,128)(2,1)S(1)} async-done(((bf16[16,128,256]{2,1,0:T(8,128)(2,1)}), bf16[16,128,256]{2,1,0:T(8,128)(2,1)S(1)}, u32[]{:S(2)}, u32[]{:S(2)}) %all-to-all-start) | async-done | bytes 1048608 | tf_op jit(solution)/shard_map/all_to_all | solution.py:256
  25.8 1.6 collective-permute-start
  27.4 0.1 slice.7
  27.5 2.2 %collective-permute-start.2 = (bf16[4,4,128,128]{3,2,1,0:T(8,128)(2,1)S(1)}, bf16[4,4,128,128]{3,2,1,0:T(8,128)(2,1)}, u32[]{:S(2)}, u32[]{:S(2)}) collective-permute-start(bf16[4,4,128,128]{3,2,1,0:T(8,128)(2,1)S(1)} %slice.7), channel_id=1, source_target_pairs={{0,24},{8,0},{16,8},{24,16},{1,25},{9,1},{17,9},{25,17},{2,26},{10... | collective-permute-start | bytes 1572872 | tf_op jit(solution)/shard_map/ppermute | solution.py:245
  29.7 4.5 %all-to-all-start.3 = ((bf16[16,128,512]{2,1,0:T(8,128)(2,1)}), bf16[16,128,512]{2,1,0:T(8,128)(2,1)}, u32[]{:S(2)}, u32[]{:S(2)}) async-start(bf16[16,128,512]{2,1,0:T(8,128)(2,1)} %get-tuple-element.14), calls=%async_computation.3 | async-start | bytes 4194304 | tf_op jit(solution)/shard_map/all_to_all | solution.py:270
  34.2 4.5 %collective-permute-done.2 = bf16[4,4,128,128]{3,2,1,0:T(8,128)(2,1)} collective-permute-done((bf16[4,4,128,128]{3,2,1,0:T(8,128)(2,1)S(1)}, bf16[4,4,128,128]{3,2,1,0:T(8,128)(2,1)}, u32[]{:S(2)}, u32[]{:S(2)}) %collective-permute-start.2) | collective-permute-done | bytes 524320 | tf_op jit(solution)/shard_map/ppermute | solution.py:245
  38.7 3.3 %collective-permute-start.3 = (bf16[4,4,128,128]{3,2,1,0:T(8,128)(2,1)}, bf16[4,4,128,128]{3,2,1,0:T(8,128)(2,1)S(1)}, u32[]{:S(2)}, u32[]{:S(2)}) collective-permute-start(bf16[4,4,128,128]{3,2,1,0:T(8,128)(2,1)} %collective-permute-done.2), channel_id=1, source_target_pairs={{0,24},{8,0},{16,8},{24,16},{1,25},{9,1},{17,9},{25,17},{2,26},{10... | collective-permute-start | bytes 1572872 | tf_op jit(solution)/shard_map/ppermute | solution.py:245
  41.9 8.7 %collective-permute-done.r_8_ = bf16[4,4,128,256]{3,2,1,0:T(8,128)(2,1)S(1)} collective-permute-done((bf16[4,4,128,256]{3,2,1,0:T(8,128)(2,1)S(1)}, bf16[4,4,128,256]{3,2,1,0:T(8,128)(2,1)S(1)}, u32[]{:S(2)}, u32[]{:S(2)}) %collective-permute-start) | collective-permute-done | bytes 1048608 | tf_op jit(solution)/shard_map/ppermute | solution.py:245
  50.6 0.9 slice.8
  51.5 11.8 %collective-permute-done.1.r_5_ = bf16[4,4,128,128]{3,2,1,0:T(8,128)(2,1)S(1)} collective-permute-done((bf16[4,4,128,128]{3,2,1,0:T(8,128)(2,1)}, bf16[4,4,128,128]{3,2,1,0:T(8,128)(2,1)S(1)}, u32[]{:S(2)}, u32[]{:S(2)}) %collective-permute-start.1) | collective-permute-done | bytes 524320 | tf_op jit(solution)/shard_map/ppermute | solution.py:245
  63.3 2.0 %broadcast_select_fusion = (bf16[4,4,128,256]{3,2,1,0:T(8,128)(2,1)}, bf16[4,4,128,256]{3,2,1,0:T(8,128)(2,1)}) fusion(bf16[4,4,128,256]{3,2,1,0:T(8,128)(2,1)S(1)} %bitcast.10, bf16[4,4,128,256]{3,2,1,0:T(8,128)(2,1)S(1)} %collective-permute-done.r_8_, pred[]{:T(512)S(6)} %eq.4, bf16[4,4,128,128]{3,2,1,0:T(8,128)(2,1)S(1)} %collective-permute-done.3.r_6_, ...), kind=kLoop, calls=%fused_computation.1 | loop fusion | flops 3145728 | bytes 5242881 | tf_op jit(solution)/shard_map/jit(_where)/select_n | solution.py:263
  65.3 3.9 %collective-permute-start.5 = (bf16[4,4,128,256]{3,2,1,0:T(8,128)(2,1)}, bf16[4,4,128,256]{3,2,1,0:T(8,128)(2,1)}, u32[]{:S(2)}, u32[]{:S(2)}) collective-permute-start(bf16[4,4,128,256]{3,2,1,0:T(8,128)(2,1)} %get-tuple-element.15), channel_id=1, source_target_pairs={{0,4},{4,0},{1,5},{5,1},{2,6},{6,2},{3,7},{7,3},{8,12},{12,8},{9,1... | collective-permute-start | bytes 3145736 | tf_op jit(solution)/shard_map/ppermute | solution.py:249
  69.2 0.1 collective-permute-start.4
  69.3 6.0 %all-to-all-start.1 = ((bf16[16,128,512]{2,1,0:T(8,128)(2,1)}), bf16[16,128,512]{2,1,0:T(8,128)(2,1)}, u32[]{:S(2)}, u32[]{:S(2)}) async-start(bf16[16,128,512]{2,1,0:T(8,128)(2,1)} %get-tuple-element.12), calls=%async_computation.1 | async-start | bytes 4194304 | tf_op jit(solution)/shard_map/all_to_all | solution.py:270
  75.4 27.5 %attend.3 = bf16[32,4,16,512]{3,2,1,0:T(8,128)(2,1)} custom-call(s32[16]{0:T(128)S(1)} %copy-done.1, s32[32,32]{1,0:T(8,128)S(1)} %copy-done, s32[1]{0:T(128)} %bitcast.r_2_, f32[512,128]{1,0:T(8,128)S(1)} %copy-done.2, bf16[4,4,128,512]{3,2,1,0:T(8,128)(2,1)} %bitcast.5.r_4_, bf16[4,4,128,128]{3,2,1,0:T(8,128)(2,1)S(1)} %collective-permute-done.1.r_5_, ...), custom_call_target="tpu_custom_call" | custom-call | flops 19327352832 | bytes 16777216 | tf_op jit(solution)/shard_map/attend/pallas_call | solution.py:160
  102.9 5.0 %all-to-all-done.1 = bf16[16,128,512]{2,1,0:T(8,128)(2,1)} async-done(((bf16[16,128,512]{2,1,0:T(8,128)(2,1)}), bf16[16,128,512]{2,1,0:T(8,128)(2,1)}, u32[]{:S(2)}, u32[]{:S(2)}) %all-to-all-start.1) | async-done | bytes 2097184 | tf_op jit(solution)/shard_map/all_to_all | solution.py:270
  107.9 5.9 %all-to-all-start.4 = ((bf16[128,16,512]{2,1,0:T(8,128)(2,1)}), bf16[128,16,512]{2,1,0:T(8,128)(2,1)}, u32[]{:S(2)}, u32[]{:S(2)}) async-start(bf16[128,16,512]{2,1,0:T(8,128)(2,1)} %bitcast.14), calls=%async_computation.4 | async-start | bytes 4194304 | tf_op jit(solution)/shard_map/all_to_all | solution.py:272
  113.8 27.4 %attend.2 = bf16[32,4,16,512]{3,2,1,0:T(8,128)(2,1)} custom-call(s32[16]{0:T(128)S(1)} %copy-done.1, s32[32,32]{1,0:T(8,128)S(1)} %copy-done, s32[1]{0:T(128)} %bitcast.r_2_, f32[512,128]{1,0:T(8,128)S(1)} %copy-done.2, bf16[4,4,128,512]{3,2,1,0:T(8,128)(2,1)} %bitcast.2.r_4_, bf16[4,4,128,128]{3,2,1,0:T(8,128)(2,1)S(1)} %collective-permute-done.1.r_5_, ...), custom_call_target="tpu_custom_call" | custom-call | flops 19327352832 | bytes 16777216 | tf_op jit(solution)/shard_map/attend/pallas_call | solution.py:160
  141.3 3.3 %all-to-all-done.4 = bf16[128,16,512]{2,1,0:T(8,128)(2,1)} async-done(((bf16[128,16,512]{2,1,0:T(8,128)(2,1)}), bf16[128,16,512]{2,1,0:T(8,128)(2,1)}, u32[]{:S(2)}, u32[]{:S(2)}) %all-to-all-start.4) | async-done | bytes 2097184 | tf_op jit(solution)/shard_map/all_to_all | solution.py:272
  144.6 38.6 %all_to_all.25 = bf16[128,16,512]{2,1,0:T(8,128)(2,1)} all-to-all(bf16[128,16,512]{2,1,0:T(8,128)(2,1)} %bitcast.15), channel_id=1, replica_groups=mesh['y'=4,'z'=4,'core'=2,'x'=4] {'y','z','core','x'}, dimensions={0} | all-to-all | bytes 4194304 | tf_op jit(solution)/shard_map/all_to_all | solution.py:272
  183.2 4.7 %place.1 = bf16[128,16384]{1,0:T(8,128)(2,1)} custom-call(bf16[4,8,4,16,512]{4,3,2,1,0:T(8,128)(2,1)} %bitcast.13, bf16[4,8,4,16,512]{4,3,2,1,0:T(8,128)(2,1)} %bitcast.7.refs_1_), custom_call_target="tpu_custom_call" | custom-call | tf_op jit(solution)/shard_map/place/pallas_call | solution.py:234
  (11 shorter events, 0.0 us)
Async XLA Ops:
  2.1 23.6 %all-to-all-start = ((bf16[16,128,256]{2,1,0:T(8,128)(2,1)}), bf16[16,128,256]{2,1,0:T(8,128)(2,1)S(1)}, u32[]{:S(2)}, u32[]{:S(2)}) async-start(bf16[16,128,256]{2,1,0:T(8,128)(2,1)} %pack.1), calls=%async_computation | async-start | bytes 2097152 | tf_op jit(solution)/shard_map/all_to_all | solution.py:256
  25.8 24.8 %collective-permute-start = (bf16[4,4,128,256]{3,2,1,0:T(8,128)(2,1)S(1)}, bf16[4,4,128,256]{3,2,1,0:T(8,128)(2,1)S(1)}, u32[]{:S(2)}, u32[]{:S(2)}) collective-permute-start(bf16[4,4,128,256]{3,2,1,0:T(8,128)(2,1)S(1)} %bitcast.8), channel_id=1, source_target_pairs={{0,8},{8,16},{16,24},{24,0},{1,9},{9,17},{17,25},{25,1},{2,10},{10... | collective-permute-start | bytes 3145736 | tf_op jit(solution)/shard_map/ppermute | solution.py:245
  27.5 11.1 %collective-permute-start.2 = (bf16[4,4,128,128]{3,2,1,0:T(8,128)(2,1)S(1)}, bf16[4,4,128,128]{3,2,1,0:T(8,128)(2,1)}, u32[]{:S(2)}, u32[]{:S(2)}) collective-permute-start(bf16[4,4,128,128]{3,2,1,0:T(8,128)(2,1)S(1)} %slice.7), channel_id=1, source_target_pairs={{0,24},{8,0},{16,8},{24,16},{1,25},{9,1},{17,9},{25,17},{2,26},{10... | collective-permute-start | bytes 1572872 | tf_op jit(solution)/shard_map/ppermute | solution.py:245
  29.7 39.6 %all-to-all-start.3 = ((bf16[16,128,512]{2,1,0:T(8,128)(2,1)}), bf16[16,128,512]{2,1,0:T(8,128)(2,1)}, u32[]{:S(2)}, u32[]{:S(2)}) async-start(bf16[16,128,512]{2,1,0:T(8,128)(2,1)} %get-tuple-element.14), calls=%async_computation.3 | async-start | bytes 4194304 | tf_op jit(solution)/shard_map/all_to_all | solution.py:270
  38.7 12.8 %collective-permute-start.3 = (bf16[4,4,128,128]{3,2,1,0:T(8,128)(2,1)}, bf16[4,4,128,128]{3,2,1,0:T(8,128)(2,1)S(1)}, u32[]{:S(2)}, u32[]{:S(2)}) collective-permute-start(bf16[4,4,128,128]{3,2,1,0:T(8,128)(2,1)} %collective-permute-done.2), channel_id=1, source_target_pairs={{0,24},{8,0},{16,8},{24,16},{1,25},{9,1},{17,9},{25,17},{2,26},{10... | collective-permute-start | bytes 1572872 | tf_op jit(solution)/shard_map/ppermute | solution.py:245
  51.5 11.8 %collective-permute-start.1 = (bf16[4,4,128,128]{3,2,1,0:T(8,128)(2,1)}, bf16[4,4,128,128]{3,2,1,0:T(8,128)(2,1)S(1)}, u32[]{:S(2)}, u32[]{:S(2)}) collective-permute-start(bf16[4,4,128,128]{3,2,1,0:T(8,128)(2,1)} %slice.8), channel_id=1, source_target_pairs={{0,8},{8,16},{16,24},{24,0},{1,9},{9,17},{17,25},{25,1},{2,10},{10... | collective-permute-start | bytes 1572872 | tf_op jit(solution)/shard_map/ppermute | solution.py:245
  65.3 10.0 %collective-permute-start.5 = (bf16[4,4,128,256]{3,2,1,0:T(8,128)(2,1)}, bf16[4,4,128,256]{3,2,1,0:T(8,128)(2,1)}, u32[]{:S(2)}, u32[]{:S(2)}) collective-permute-start(bf16[4,4,128,256]{3,2,1,0:T(8,128)(2,1)} %get-tuple-element.15), channel_id=1, source_target_pairs={{0,4},{4,0},{1,5},{5,1},{2,6},{6,2},{3,7},{7,3},{8,12},{12,8},{9,1... | collective-permute-start | bytes 3145736 | tf_op jit(solution)/shard_map/ppermute | solution.py:249
  69.2 6.1 %copy-start = (s32[32,32]{1,0:T(8,128)S(1)}, s32[32,32]{1,0:T(8,128)}, u32[]{:S(2)}) copy-start(s32[32,32]{1,0:T(8,128)} %r_1_.3) | copy-start | bytes 12292
  69.2 6.2 %copy-start.1 = (s32[16]{0:T(128)S(1)}, s32[16]{0:T(128)}, u32[]{:S(2)}) copy-start(s32[16]{0:T(128)} %r_0_.3) | copy-start | bytes 196
  69.2 6.2 %copy-start.2 = (f32[512,128]{1,0:T(8,128)S(1)}, f32[512,128]{1,0:T(8,128)}, u32[]{:S(2)}) copy-start(f32[512,128]{1,0:T(8,128)} %constant.16.clone.r_3_) | copy-start | bytes 786436
  69.2 6.1 %collective-permute-start.4 = (bf16[4,4,128,256]{3,2,1,0:T(8,128)(2,1)}, bf16[4,4,128,256]{3,2,1,0:T(8,128)(2,1)}, u32[]{:S(2)}, u32[]{:S(2)}) collective-permute-start(bf16[4,4,128,256]{3,2,1,0:T(8,128)(2,1)} %get-tuple-element.16), channel_id=1, source_target_pairs={{0,4},{4,0},{1,5},{5,1},{2,6},{6,2},{3,7},{7,3},{8,12},{12,8},{9,1... | collective-permute-start | bytes 3145736 | tf_op jit(solution)/shard_map/ppermute | solution.py:249
  69.3 38.6 %all-to-all-start.1 = ((bf16[16,128,512]{2,1,0:T(8,128)(2,1)}), bf16[16,128,512]{2,1,0:T(8,128)(2,1)}, u32[]{:S(2)}, u32[]{:S(2)}) async-start(bf16[16,128,512]{2,1,0:T(8,128)(2,1)} %get-tuple-element.12), calls=%async_computation.1 | async-start | bytes 4194304 | tf_op jit(solution)/shard_map/all_to_all | solution.py:270
  107.9 36.6 %all-to-all-start.4 = ((bf16[128,16,512]{2,1,0:T(8,128)(2,1)}), bf16[128,16,512]{2,1,0:T(8,128)(2,1)}, u32[]{:S(2)}, u32[]{:S(2)}) async-start(bf16[128,16,512]{2,1,0:T(8,128)(2,1)} %bitcast.14), calls=%async_computation.4 | async-start | bytes 4194304 | tf_op jit(solution)/shard_map/all_to_all | solution.py:272

commit v2 on v1

v2 whole, which is shorter than its diff:
```python
import functools
import math
import jax, jax.numpy as jnp, numpy as np
from jax import lax
from jax.experimental import pallas as pl
from jax.experimental.pallas import tpu as pltpu
from jax.sharding import PartitionSpec as P

HD = 128
BLOCK = 512
REACH = 2048
TILE = 256
KEYS = 256
BIG = float(2 ** 20)
NDOC = 16
SEQ = 16384


def scaled_frequencies(head_width):
    exponents = np.arange(0, head_width, 2) / head_width
    inverse = 1.0 / np.power(500000.0, exponents)
    wavelength = 2.0 * np.pi / inverse
    smooth = (8192.0 / wavelength - 1.0) / 3.0
    blended = (1.0 - smooth) * inverse / 8.0 + smooth * inverse
    middle = np.where(wavelength > 8192.0, inverse / 8.0, blended)
    return np.where(wavelength < 2048.0, inverse, middle)


def rotation_tables():
    f = scaled_frequencies(HD)
    coarse = np.arange(SEQ // 128)[:, None] * 128.0 * f[None, :]
    fine = np.arange(128)[:, None] * 1.0 * f[None, :]
    parts = (np.cos(coarse), np.sin(coarse), np.cos(fine), np.sin(fine))
    return np.concatenate([np.concatenate([p, p], axis=1) for p in parts], axis=0).astype(np.float32)


def tables(tab, u):
    sign = jnp.where(lax.broadcasted_iota(jnp.int32, (1, 128), 1) < 64, -1.0, 1.0)
    C = tab[pl.ds(u, 1), :]
    S = tab[pl.ds(u + 128, 1), :]
    c = tab[256:384, :]
    n = tab[384:512, :]
    return C * c - S * n, (S * c + C * n) * sign


def rotated(x, cos, sin):
    x = x.astype(jnp.float32)
    return (x * cos + pltpu.roll(x, 64, 1) * sin).astype(jnp.bfloat16)


def attn_kernel(heads, doc_ref, plan_ref, at_ref, q_ref, k4, v4, k3, k2, k1, k0, out_ref, kaug, vt, qs, inv):
    s = pl.program_id(0) * 8 + at_ref[0]
    lane = lax.broadcasted_iota(jnp.int32, (1, 128), 1)
    first_token = s * BLOCK
    starts = jnp.zeros((1, 128), jnp.int32)
    ends = jnp.zeros((1, 128), jnp.int32)
    bounds = []
    begin = jnp.int32(0)
    for d in range(NDOC):
        bounds.append(begin)
        end = begin + doc_ref[d]
        starts = jnp.where(lane == d, begin, starts)
        ends = jnp.where(lane == d, end, ends)
        begin = end
    starts = jnp.where(lane == NDOC, -(1 << 20), starts)

    def note(r, c):
        inv[plan_ref[s, r]] = r
        return c

    lax.fori_loop(0, 32, note, 0)
    def inside(pos):
        p = pos + lax.broadcasted_iota(jnp.int32, (128, 128), 0)
        return (p >= starts) & (p < ends)

    base = first_token - REACH
    scale = math.log2(math.e) / math.sqrt(HD)
    spans = []
    for t in range(BLOCK // TILE):
        pos = first_token + t * TILE
        low = jnp.int32(0)
        for d in range(NDOC):
            low = jnp.where(bounds[d] <= pos, bounds[d], low)
        need = (pos + TILE - low + KEYS - 1) // KEYS
        span = jnp.int32(SPANS[-1])
        for n in reversed(SPANS[:-1]):
            span = jnp.where(need <= n, n, span)
        spans.append(span)
    lowest = functools.reduce(
        jnp.minimum, [REACH + TILE * (t + 1) - KEYS * spans[t] for t in range(BLOCK // TILE)])

    vt[128:144, :] = jnp.ones((16, REACH + BLOCK), jnp.bfloat16)
    for b, (kr, vr, vc) in enumerate(
            ((k4, v4, 0), (k3, k3, 128), (k2, k2, 128), (k1, k1, 128), (k0, k0, 128))):
        @pl.when((b + 1) * BLOCK > lowest)
        def _(b=b, kr=kr, vr=vr, vc=vc):
            for i in range(4):
                pos = base + b * BLOCK + i * 128
                at = b * BLOCK + i * 128
                kaug[at:at + 128, 0:128] = kr[0, i, :, 0:128]
                kaug[at:at + 128, 128:256] = jnp.where(inside(pos), 1.0, 0.0).astype(jnp.bfloat16)
                vt[0:128, at:at + 128] = vr[0, i, :, vc:vc + 128]

    def score(start, h, n):
        sc = lax.dot_general(kaug[pl.ds(start, KEYS * n), :], qs[h * TILE:h * TILE + TILE, :],
                             (((1,), (1,)), ((), ())), preferred_element_type=jnp.float32)
        key = lax.broadcasted_iota(jnp.int32, (KEYS, TILE), 0)
        tok = lax.broadcasted_iota(jnp.int32, (KEYS, TILE), 1)
        parts = [sc[KEYS * k:KEYS * k + KEYS] for k in range(n)]
        parts[-1] = jnp.where(key <= tok, parts[-1], -1e30)
        high = functools.reduce(jnp.maximum, [jnp.max(x, axis=0, keepdims=True) for x in parts])
        return parts, high

    def mix(start, t, h, n, parts, high):
        p = [jnp.exp2((x - high) * scale).astype(jnp.bfloat16) for x in parts]
        got = lax.dot_general(vt[:, pl.ds(start, KEYS * n)], jnp.concatenate(p, axis=0),
                              (((1,), (0,)), ((), ())), preferred_element_type=jnp.float32)
        o = (got[0:128] * (1.0 / got[128:129])).T.astype(jnp.bfloat16)
        for i in range(TILE // 16):
            out_ref[inv[t * (TILE // 16) + i], 0, :, h * 128:h * 128 + 128] = o[i * 16:i * 16 + 16]

    def tile(t, carry):
        for u in range(TILE // 128):
            pos = first_token + t * TILE + u * 128
            bias = jnp.where(inside(pos), 0.0, -BIG).astype(jnp.bfloat16)
            for h in range(heads):
                at = h * TILE + u * 128
                qs[at:at + 128, 0:128] = q_ref[0, t * (TILE // 128) + u, :, h * 128:h * 128 + 128]
                qs[at:at + 128, 128:256] = bias
        span = jnp.where(t == 0, spans[0], spans[1])

        def run(n):
            start = pl.multiple_of(REACH + TILE * (t + 1) - KEYS * n, 256)
            got = {}
            for h in range(heads + AHEAD):
                if h < heads:
                    got[h] = score(start, h, n)
                if h >= AHEAD:
                    mix(start, t, h - AHEAD, n, *got.pop(h - AHEAD))

        for n in SPANS:
            pl.when(span == n)(functools.partial(run, n))
        return carry

    lax.fori_loop(0, BLOCK // TILE, tile, 0)


AHEAD = 3
SPANS = (1, 2, 3, 4, 5, 7, 9)


def attend(heads, docs, plan, at, q, kv):
    smem = pl.BlockSpec(memory_space=pltpu.SMEM)

    def back(d, width):
        def index(y, docs_ref, plan_ref, at_ref):
            return (jnp.maximum(jnp.where(at_ref[0] < d, y - 1, y), 0), 0, 0, 0)

        return pl.BlockSpec((1, 4, 128, width), index)

    work = 16 * heads * 128 * 9 * 256 * 2 * 512
    return pl.pallas_call(
        lambda *r: attn_kernel(heads, *r),
        out_shape=jax.ShapeDtypeStruct((32, 4, 16, heads * 128), jnp.bfloat16),
        grid_spec=pltpu.PrefetchScalarGridSpec(
            num_scalar_prefetch=3,
            grid=(4,),
            in_specs=[
                pl.BlockSpec((1, 4, 128, heads * 128), lambda y, *_: (y, 0, 0, 0)),
            ] + [back(4, 128), back(4, 128), back(3, 256), back(2, 256), back(1, 256), back(0, 256)],
            out_specs=pl.BlockSpec((32, 1, 16, heads * 128), lambda y, *_: (0, y, 0, 0)),
            scratch_shapes=[
                pltpu.VMEM((REACH + BLOCK, 256), jnp.bfloat16),
                pltpu.VMEM((144, REACH + BLOCK), jnp.bfloat16),
                pltpu.VMEM((heads * TILE, 256), jnp.bfloat16),
                pltpu.SMEM((32,), jnp.int32),
            ],
        ),
        compiler_params=pltpu.CompilerParams(vmem_limit_bytes=48 << 20),
        cost_estimate=pl.CostEstimate(flops=work, bytes_accessed=16 << 20, transcendentals=0),
        name="attend",
    )(docs, plan, at, q, *kv)


AXES = ("y", "z", "core", "x")
CHUNKS = 2


def pack_kernel(seat, tab, keys, values, out):
    cos, sin = tables(tab, seat[0])
    for g in range(8):
        k = rotated(keys[:, g * 128:g * 128 + 128], cos, sin)
        v = values[:, g * 128:g * 128 + 128].T
        for twin in range(2):
            out[2 * g + twin, :, 0:128] = k
            out[2 * g + twin, :, 128:256] = v


def pack(seat, tab, keys, values):
    return pl.pallas_call(
        pack_kernel,
        out_shape=jax.ShapeDtypeStruct((16, 128, 256), jnp.bfloat16),
        in_specs=[pl.BlockSpec(memory_space=pltpu.SMEM)] + [pl.BlockSpec(memory_space=pltpu.VMEM)] * 3,
        name="pack",
    )(seat, tab, keys, values)


def split_kernel(seat, tab, rows, *outs):
    cos, sin = tables(tab, seat[0])
    count = 8 // len(outs)
    for g in range(4):
        for j, out in enumerate(outs):
            for h in range(count):
                col = g * 1024 + (j * count + h) * 128
                out[g, :, h * 128:h * 128 + 128] = rotated(rows[:, col:col + 128], cos, sin)


def split(seat, tab, rows):
    width = 1024 // CHUNKS
    return pl.pallas_call(
        split_kernel,
        grid=(4,),
        out_shape=[jax.ShapeDtypeStruct((16, 128, width), jnp.bfloat16)] * CHUNKS,
        in_specs=[
            pl.BlockSpec(memory_space=pltpu.SMEM),
            pl.BlockSpec((512, 128), lambda g: (0, 0)),
            pl.BlockSpec((128, 4096), lambda g: (0, g)),
        ],
        out_specs=[pl.BlockSpec((4, 128, width), lambda g: (g, 0, 0))] * CHUNKS,
        cost_estimate=pl.CostEstimate(flops=2 << 30, bytes_accessed=8 << 20, transcendentals=0),
        name="split",
    )(seat, tab, rows)


def place_kernel(chunk, part, *refs):
    out, sem = refs[-2:]
    width = 1024 // CHUNKS
    copies = []
    for y in range(4):
        for b in range(8):
            for x in range(4):
                copies.append(pltpu.make_async_copy(
                    part.at[y, b, x],
                    out.at[pl.ds(b * 16, 16), pl.ds((y * 4 + x) * 1024 + chunk * width, width)],
                    sem.at[len(copies)]))
    for c in copies:
        c.start()
    for c in copies:
        c.wait()


def place(chunk, part, rows):
    before = [] if rows is None else [rows]
    return pl.pallas_call(
        functools.partial(place_kernel, chunk),
        out_shape=jax.ShapeDtypeStruct((128, 16384), jnp.bfloat16),
        in_specs=[pl.BlockSpec(memory_space=pltpu.VMEM)] + [pl.BlockSpec(memory_space=pl.ANY)] * len(before),
        out_specs=pl.BlockSpec(memory_space=pl.ANY),
        scratch_shapes=[pltpu.SemaphoreType.DMA((128,))],
        input_output_aliases={1: 0} if before else {},
        name="place",
    )(part, *before)


def ring(a, by):
    return lax.ppermute(a, "z", [(i, (i + by) % 4) for i in range(4)])


def swap(a):
    return lax.ppermute(a, "core", [(0, 1), (1, 0)])


def on_device(query_rows, token_keys, token_values, doc_lengths, block_plan):
    at = (lax.axis_index("z") * 2 + lax.axis_index("core")).astype(jnp.int32).reshape(1)
    core = lax.axis_index("core")
    seat = ((lax.axis_index("y") * 8 + at[0]) * 4 + lax.axis_index("x")).astype(jnp.int32).reshape(1)
    tab = jnp.asarray(rotation_tables())
    kv = pack(seat, tab, token_keys, token_values)
    own = lax.all_to_all(kv, ("y", "x"), split_axis=0, concat_axis=0, tiled=True).reshape(4, 4, 128, 256)
    parts = split(seat, tab, query_rows)
    own, *parts = lax.optimization_barrier((own, *parts))
    near = ring(own, 1)
    left_values = ring(own[..., 128:], -1)
    far_keys = ring(near[..., :128], 1)
    far_values = ring(left_values, -1)
    first = swap(jnp.where(core == 0, own, near))
    third = swap(jnp.where(core == 0, near, jnp.concatenate([far_keys, far_values], axis=-1)))
    kv = (far_keys, far_values, third, near, first, own)
    width = 1024 // CHUNKS
    rows = None
    for j, part in enumerate(parts):
        part = lax.all_to_all(part, ("y", "x"), split_axis=0, concat_axis=0, tiled=True)
        o = attend(8 // CHUNKS, doc_lengths, block_plan, at, part.reshape(4, 4, 128, width), kv)
        o = lax.all_to_all(o.reshape(128, 16, width), AXES, split_axis=0, concat_axis=0, tiled=True)
        rows = place(j, o.reshape(4, 8, 4, 16, width), rows)
    return rows


def solution(mesh):
    fine = jax.sharding.Mesh(mesh.devices.reshape(4, 4, 2, 4), AXES)
    rows = P(AXES, None)
    return jax.shard_map(
        on_device, mesh=fine, in_specs=(rows, rows, rows, P(), P()), out_specs=rows, check_vma=False
    )
```

time: 189 us -> 186 us (0.984)
  waiting for transfers between devices: 44.6 us -> 84.2 us
  blocking collectives: 38.6 us -> 0 us
  Pallas kernels: 66.5 us -> 56.7 us
  starting transfers between devices: 35 us -> 40.4 us
    all_to_all x1 -> x0, blocking collectives: 38.6 us -> none  [on_device(): lax.all_to_all(o.reshape(128, 16, width), AXES, split_axis=0, concat_axis...]
    all_to_all x1 -> x2, waiting for transfers between devices: 3.29 us -> 37.3 us  [on_device(): lax.all_to_all(o.reshape(128, 16, width), AXES, split_axis=0, concat_axis...]
    pallas_call x2, Pallas kernels: 54.9 us -> 40.7 us  [attend(): pl.pallas_call(lambda *r: attn_kernel(heads, *r), out_shape=jax.ShapeDtyp...]
    all_to_all x2, waiting for transfers between devices: 5.04 us -> 11.5 us  [on_device(): lax.all_to_all(part, ('y', 'x'), split_axis=0, concat_axis=0, tiled=True)]
    all_to_all x1 -> x2, starting transfers between devices: 5.9 us -> 11.4 us  [on_device(): lax.all_to_all(o.reshape(128, 16, width), AXES, split_axis=0, concat_axis...]
    pallas_call x1 -> x2, Pallas kernels: 4.68 us -> 8.02 us  [place(): pl.pallas_call(functools.partial(place_kernel, chunk), out_shape=jax.Shap...]
  transfers between devices with their start and end apart: 10 -> 11, of which waited for: 6 -> 7; matrix products, arithmetic and copies ran while one was open for 2% -> 2% of each run, Pallas kernels for 32% -> 27%
where the time goes in v2:
time: 186 us
  waiting for transfers between devices  84.2 us (45%)
  Pallas kernels  56.7 us (30%)
  starting transfers between devices  40.4 us (22%)
  local copies, waits for them, and re-layouts  2.33 us (1%)
  other arithmetic  1.97 us (1%)
    pallas_call x2, Pallas kernels, attend(): pl.pallas_call(lambda *r: attn_kernel(heads, *r), out_shape=jax.ShapeDtyp...  40.7 us
    all_to_all x2, waiting for transfers between devices, on_device(): lax.all_to_all(o.reshape(128, 16, width), AXES, split_axis=0, concat_axis...  37.3 us
    ppermute x4, waiting for transfers between devices, ring(): return lax.ppermute(a, 'z', [(i, (i + by) % 4) for i in range(4)])  25 us
    all_to_all x2, waiting for transfers between devices, on_device(): lax.all_to_all(part, ('y', 'x'), split_axis=0, concat_axis=0, tiled=True)  11.5 us
    all_to_all x2, starting transfers between devices, on_device(): lax.all_to_all(o.reshape(128, 16, width), AXES, split_axis=0, concat_axis...  11.4 us
    all_to_all x2, starting transfers between devices, on_device(): lax.all_to_all(part, ('y', 'x'), split_axis=0, concat_axis=0, tiled=True)  10.3 us
    all_to_all x1, waiting for transfers between devices, on_device(): lax.all_to_all(kv, ('y', 'x'), split_axis=0, concat_axis=0, tiled=True)  10.3 us
    pallas_call x2, Pallas kernels, place(): pl.pallas_call(functools.partial(place_kernel, chunk), out_shape=jax.Shap...  8.02 us
  transfers between devices with their start and end apart: 11, of which 7 were waited for; matrix products, arithmetic and copies ran while one was open for 2% of the time, Pallas kernels for 27%

profile of v2, /device:TPU:1, one launch (start us, length us, event | category | flops | bytes accessed | tf_op | source)
XLA Modules:
  0.0 185.9 jit_solution(17598689081449399910)
XLA Ops:
  0.0 2.3 %pack.1 = bf16[16,128,256]{2,1,0:T(8,128)(2,1)} custom-call(s32[1]{0:T(128)} %bitcast.1.seat, f32[512,128]{1,0:T(8,128)} %constant.26.clone.tab, bf16[128,1024]{1,0:T(8,128)(2,1)} %keys.1, bf16[128,1024]{1,0:T(8,128)(2,1)} %values.1), custom_call_target="tpu_custom_call" | custom-call | tf_op jit(solution)/shard_map/pack/pallas_call | solution.py:200
  2.3 7.6 %all-to-all-start = ((bf16[16,128,256]{2,1,0:T(8,128)(2,1)}), bf16[16,128,256]{2,1,0:T(8,128)(2,1)S(1)}, u32[]{:S(2)}, u32[]{:S(2)}) async-start(bf16[16,128,256]{2,1,0:T(8,128)(2,1)} %pack.1), calls=%async_computation | async-start | bytes 2097152 | tf_op jit(solution)/shard_map/all_to_all | solution.py:279
  9.9 5.7 %split.1 = (bf16[16,128,512]{2,1,0:T(8,128)(2,1)}, bf16[16,128,512]{2,1,0:T(8,128)(2,1)}) custom-call(s32[1]{0:T(128)} %bitcast.1.seat, f32[512,128]{1,0:T(8,128)} %constant.26.clone.tab, bf16[128,16384]{1,0:T(8,128)(2,1)} %rows.1), custom_call_target="tpu_custom_call" | custom-call | flops 2147483648 | bytes 8388608 | tf_op jit(solution)/shard_map/split/pallas_call | solution.py:220
  15.6 10.3 %all-to-all-done = bf16[16,128,256]{2,1,0:T(8,128)(2,1)S(1)} async-done(((bf16[16,128,256]{2,1,0:T(8,128)(2,1)}), bf16[16,128,256]{2,1,0:T(8,128)(2,1)S(1)}, u32[]{:S(2)}, u32[]{:S(2)}) %all-to-all-start) | async-done | bytes 1048608 | tf_op jit(solution)/shard_map/all_to_all | solution.py:279
  25.9 1.6 collective-permute-start
  27.7 2.2 %collective-permute-start.2 = (bf16[4,4,128,128]{3,2,1,0:T(8,128)(2,1)S(1)}, bf16[4,4,128,128]{3,2,1,0:T(8,128)(2,1)}, u32[]{:S(2)}, u32[]{:S(2)}) collective-permute-start(bf16[4,4,128,128]{3,2,1,0:T(8,128)(2,1)S(1)} %slice.7), channel_id=1, source_target_pairs={{0,24},{8,0},{16,8},{24,16},{1,25},{9,1},{17,9},{25,17},{2,26},{10... | collective-permute-start | bytes 1572872 | tf_op jit(solution)/shard_map/ppermute | solution.py:266
  29.9 4.4 %all-to-all-start.3 = ((bf16[16,128,512]{2,1,0:T(8,128)(2,1)}), bf16[16,128,512]{2,1,0:T(8,128)(2,1)}, u32[]{:S(2)}, u32[]{:S(2)}) async-start(bf16[16,128,512]{2,1,0:T(8,128)(2,1)} %get-tuple-element.14), calls=%async_computation.3 | async-start | bytes 4194304 | tf_op jit(solution)/shard_map/all_to_all | solution.py:292
  34.3 4.5 %collective-permute-done.2 = bf16[4,4,128,128]{3,2,1,0:T(8,128)(2,1)} collective-permute-done((bf16[4,4,128,128]{3,2,1,0:T(8,128)(2,1)S(1)}, bf16[4,4,128,128]{3,2,1,0:T(8,128)(2,1)}, u32[]{:S(2)}, u32[]{:S(2)}) %collective-permute-start.2) | collective-permute-done | bytes 524320 | tf_op jit(solution)/shard_map/ppermute | solution.py:266
  38.8 3.3 %collective-permute-start.3 = (bf16[4,4,128,128]{3,2,1,0:T(8,128)(2,1)}, bf16[4,4,128,128]{3,2,1,0:T(8,128)(2,1)S(1)}, u32[]{:S(2)}, u32[]{:S(2)}) collective-permute-start(bf16[4,4,128,128]{3,2,1,0:T(8,128)(2,1)} %collective-permute-done.2), channel_id=1, source_target_pairs={{0,24},{8,0},{16,8},{24,16},{1,25},{9,1},{17,9},{25,17},{2,26},{10... | collective-permute-start | bytes 1572872 | tf_op jit(solution)/shard_map/ppermute | solution.py:266
  42.1 8.7 %collective-permute-done.r_7_ = bf16[4,4,128,256]{3,2,1,0:T(8,128)(2,1)S(1)} collective-permute-done((bf16[4,4,128,256]{3,2,1,0:T(8,128)(2,1)S(1)}, bf16[4,4,128,256]{3,2,1,0:T(8,128)(2,1)S(1)}, u32[]{:S(2)}, u32[]{:S(2)}) %collective-permute-start) | collective-permute-done | bytes 1048608 | tf_op jit(solution)/shard_map/ppermute | solution.py:266
  51.7 11.8 %collective-permute-done.1.r_4_ = bf16[4,4,128,128]{3,2,1,0:T(8,128)(2,1)S(1)} collective-permute-done((bf16[4,4,128,128]{3,2,1,0:T(8,128)(2,1)}, bf16[4,4,128,128]{3,2,1,0:T(8,128)(2,1)S(1)}, u32[]{:S(2)}, u32[]{:S(2)}) %collective-permute-start.1) | collective-permute-done | bytes 524320 | tf_op jit(solution)/shard_map/ppermute | solution.py:266
  63.5 2.0 %broadcast_select_fusion = (bf16[4,4,128,256]{3,2,1,0:T(8,128)(2,1)}, bf16[4,4,128,256]{3,2,1,0:T(8,128)(2,1)}) fusion(bf16[4,4,128,256]{3,2,1,0:T(8,128)(2,1)S(1)} %bitcast.11, bf16[4,4,128,256]{3,2,1,0:T(8,128)(2,1)S(1)} %collective-permute-done.r_7_, pred[]{:T(512)S(6)} %eq.4, bf16[4,4,128,128]{3,2,1,0:T(8,128)(2,1)S(1)} %collective-permute-done.3.r_5_, ...), kind=kLoop, calls=%fused_computation.1 | loop fusion | flops 3145728 | bytes 5242881 | tf_op jit(solution)/shard_map/jit(_where)/select_n | solution.py:286
  65.5 3.9 %collective-permute-start.5 = (bf16[4,4,128,256]{3,2,1,0:T(8,128)(2,1)}, bf16[4,4,128,256]{3,2,1,0:T(8,128)(2,1)}, u32[]{:S(2)}, u32[]{:S(2)}) collective-permute-start(bf16[4,4,128,256]{3,2,1,0:T(8,128)(2,1)} %get-tuple-element.15), channel_id=1, source_target_pairs={{0,4},{4,0},{1,5},{5,1},{2,6},{6,2},{3,7},{7,3},{8,12},{12,8},{9,1... | collective-permute-start | bytes 3145736 | tf_op jit(solution)/shard_map/ppermute | solution.py:270
  69.5 5.9 %all-to-all-start.1 = ((bf16[16,128,512]{2,1,0:T(8,128)(2,1)}), bf16[16,128,512]{2,1,0:T(8,128)(2,1)}, u32[]{:S(2)}, u32[]{:S(2)}) async-start(bf16[16,128,512]{2,1,0:T(8,128)(2,1)} %get-tuple-element.12), calls=%async_computation.1 | async-start | bytes 4194304 | tf_op jit(solution)/shard_map/all_to_all | solution.py:292
  75.4 20.3 %attend.3 = bf16[32,4,16,512]{3,2,1,0:T(8,128)(2,1)} custom-call(s32[16]{0:T(128)S(1)} %copy-done.1, s32[32,32]{1,0:T(8,128)S(1)} %copy-done, s32[1]{0:T(128)} %bitcast.r_2_, bf16[4,4,128,512]{3,2,1,0:T(8,128)(2,1)} %bitcast.6.r_3_, bf16[4,4,128,128]{3,2,1,0:T(8,128)(2,1)S(1)} %collective-permute-done.1.r_4_, ...), custom_call_target="tpu_custom_call" | custom-call | flops 19327352832 | bytes 16777216 | tf_op jit(solution)/shard_map/attend/pallas_call | solution.py:162
  95.7 11.5 %all-to-all-done.1 = bf16[16,128,512]{2,1,0:T(8,128)(2,1)} async-done(((bf16[16,128,512]{2,1,0:T(8,128)(2,1)}), bf16[16,128,512]{2,1,0:T(8,128)(2,1)}, u32[]{:S(2)}, u32[]{:S(2)}) %all-to-all-start.1) | async-done | bytes 2097184 | tf_op jit(solution)/shard_map/all_to_all | solution.py:292
  107.2 6.2 %all-to-all-start.4 = ((bf16[128,16,512]{2,1,0:T(8,128)(2,1)}), bf16[128,16,512]{2,1,0:T(8,128)(2,1)}, u32[]{:S(2)}, u32[]{:S(2)}) async-start(bf16[128,16,512]{2,1,0:T(8,128)(2,1)} %bitcast.15), calls=%async_computation.4 | async-start | bytes 4194304 | tf_op jit(solution)/shard_map/all_to_all | solution.py:294
  113.5 20.4 %attend.2 = bf16[32,4,16,512]{3,2,1,0:T(8,128)(2,1)} custom-call(s32[16]{0:T(128)S(1)} %copy-done.1, s32[32,32]{1,0:T(8,128)S(1)} %copy-done, s32[1]{0:T(128)} %bitcast.r_2_, bf16[4,4,128,512]{3,2,1,0:T(8,128)(2,1)} %bitcast.3.r_3_, bf16[4,4,128,128]{3,2,1,0:T(8,128)(2,1)S(1)} %collective-permute-done.1.r_4_, ...), custom_call_target="tpu_custom_call" | custom-call | flops 19327352832 | bytes 16777216 | tf_op jit(solution)/shard_map/attend/pallas_call | solution.py:162
  133.9 10.4 %all-to-all-done.4 = bf16[128,16,512]{2,1,0:T(8,128)(2,1)} async-done(((bf16[128,16,512]{2,1,0:T(8,128)(2,1)}), bf16[128,16,512]{2,1,0:T(8,128)(2,1)}, u32[]{:S(2)}, u32[]{:S(2)}) %all-to-all-start.4) | async-done | bytes 2097184 | tf_op jit(solution)/shard_map/all_to_all | solution.py:294
  144.2 5.1 %all-to-all-start.2 = ((bf16[128,16,512]{2,1,0:T(8,128)(2,1)}), bf16[128,16,512]{2,1,0:T(8,128)(2,1)S(1)}, u32[]{:S(2)}, u32[]{:S(2)}) async-start(bf16[128,16,512]{2,1,0:T(8,128)(2,1)} %bitcast.16), calls=%async_computation.2 | async-start | bytes 4194304 | tf_op jit(solution)/shard_map/all_to_all | solution.py:294
  149.4 4.0 %place.2.refs_0_ = bf16[128,16384]{1,0:T(8,128)(2,1)} custom-call(bf16[4,8,4,16,512]{4,3,2,1,0:T(8,128)(2,1)} %bitcast.8.part), custom_call_target="tpu_custom_call" | custom-call | tf_op jit(solution)/shard_map/place/pallas_call | solution.py:254
  153.4 26.9 %all-to-all-done.2 = bf16[128,16,512]{2,1,0:T(8,128)(2,1)S(1)} async-done(((bf16[128,16,512]{2,1,0:T(8,128)(2,1)}), bf16[128,16,512]{2,1,0:T(8,128)(2,1)S(1)}, u32[]{:S(2)}, u32[]{:S(2)}) %all-to-all-start.2) | async-done | bytes 2097184 | tf_op jit(solution)/shard_map/all_to_all | solution.py:294
  180.4 1.3 copy-done.2
  181.7 4.0 %place.3 = bf16[128,16384]{1,0:T(8,128)(2,1)} custom-call(bf16[4,8,4,16,512]{4,3,2,1,0:T(8,128)(2,1)} %bitcast.14, bf16[128,16384]{1,0:T(8,128)(2,1)} %place.2.refs_0_), custom_call_target="tpu_custom_call", output_to_operand_aliasing={{}: (1, {})} | custom-call | tf_op jit(solution)/shard_map/place/pallas_call | solution.py:254
  (13 shorter events, 1.1 us)
Async XLA Ops:
  2.3 23.6 %all-to-all-start = ((bf16[16,128,256]{2,1,0:T(8,128)(2,1)}), bf16[16,128,256]{2,1,0:T(8,128)(2,1)S(1)}, u32[]{:S(2)}, u32[]{:S(2)}) async-start(bf16[16,128,256]{2,1,0:T(8,128)(2,1)} %pack.1), calls=%async_computation | async-start | bytes 2097152 | tf_op jit(solution)/shard_map/all_to_all | solution.py:279
  25.9 24.8 %collective-permute-start = (bf16[4,4,128,256]{3,2,1,0:T(8,128)(2,1)S(1)}, bf16[4,4,128,256]{3,2,1,0:T(8,128)(2,1)S(1)}, u32[]{:S(2)}, u32[]{:S(2)}) collective-permute-start(bf16[4,4,128,256]{3,2,1,0:T(8,128)(2,1)S(1)} %bitcast.9), channel_id=1, source_target_pairs={{0,8},{8,16},{16,24},{24,0},{1,9},{9,17},{17,25},{25,1},{2,10},{10... | collective-permute-start | bytes 3145736 | tf_op jit(solution)/shard_map/ppermute | solution.py:266
  27.7 11.1 %collective-permute-start.2 = (bf16[4,4,128,128]{3,2,1,0:T(8,128)(2,1)S(1)}, bf16[4,4,128,128]{3,2,1,0:T(8,128)(2,1)}, u32[]{:S(2)}, u32[]{:S(2)}) collective-permute-start(bf16[4,4,128,128]{3,2,1,0:T(8,128)(2,1)S(1)} %slice.7), channel_id=1, source_target_pairs={{0,24},{8,0},{16,8},{24,16},{1,25},{9,1},{17,9},{25,17},{2,26},{10... | collective-permute-start | bytes 1572872 | tf_op jit(solution)/shard_map/ppermute | solution.py:266
  29.9 39.6 %all-to-all-start.3 = ((bf16[16,128,512]{2,1,0:T(8,128)(2,1)}), bf16[16,128,512]{2,1,0:T(8,128)(2,1)}, u32[]{:S(2)}, u32[]{:S(2)}) async-start(bf16[16,128,512]{2,1,0:T(8,128)(2,1)} %get-tuple-element.14), calls=%async_computation.3 | async-start | bytes 4194304 | tf_op jit(solution)/shard_map/all_to_all | solution.py:292
  38.8 12.8 %collective-permute-start.3 = (bf16[4,4,128,128]{3,2,1,0:T(8,128)(2,1)}, bf16[4,4,128,128]{3,2,1,0:T(8,128)(2,1)S(1)}, u32[]{:S(2)}, u32[]{:S(2)}) collective-permute-start(bf16[4,4,128,128]{3,2,1,0:T(8,128)(2,1)} %collective-permute-done.2), channel_id=1, source_target_pairs={{0,24},{8,0},{16,8},{24,16},{1,25},{9,1},{17,9},{25,17},{2,26},{10... | collective-permute-start | bytes 1572872 | tf_op jit(solution)/shard_map/ppermute | solution.py:266
  51.6 11.8 %collective-permute-start.1 = (bf16[4,4,128,128]{3,2,1,0:T(8,128)(2,1)}, bf16[4,4,128,128]{3,2,1,0:T(8,128)(2,1)S(1)}, u32[]{:S(2)}, u32[]{:S(2)}) collective-permute-start(bf16[4,4,128,128]{3,2,1,0:T(8,128)(2,1)} %slice.8), channel_id=1, source_target_pairs={{0,8},{8,16},{16,24},{24,0},{1,9},{9,17},{17,25},{25,1},{2,10},{10... | collective-permute-start | bytes 1572872 | tf_op jit(solution)/shard_map/ppermute | solution.py:266
  65.5 9.9 %collective-permute-start.5 = (bf16[4,4,128,256]{3,2,1,0:T(8,128)(2,1)}, bf16[4,4,128,256]{3,2,1,0:T(8,128)(2,1)}, u32[]{:S(2)}, u32[]{:S(2)}) collective-permute-start(bf16[4,4,128,256]{3,2,1,0:T(8,128)(2,1)} %get-tuple-element.15), channel_id=1, source_target_pairs={{0,4},{4,0},{1,5},{5,1},{2,6},{6,2},{3,7},{7,3},{8,12},{12,8},{9,1... | collective-permute-start | bytes 3145736 | tf_op jit(solution)/shard_map/ppermute | solution.py:270
  69.4 6.0 %copy-start = (s32[32,32]{1,0:T(8,128)S(1)}, s32[32,32]{1,0:T(8,128)}, u32[]{:S(2)}) copy-start(s32[32,32]{1,0:T(8,128)} %r_1_.3) | copy-start | bytes 12292
  69.4 6.0 %copy-start.1 = (s32[16]{0:T(128)S(1)}, s32[16]{0:T(128)}, u32[]{:S(2)}) copy-start(s32[16]{0:T(128)} %r_0_.3) | copy-start | bytes 196
  69.4 6.0 %collective-permute-start.4 = (bf16[4,4,128,256]{3,2,1,0:T(8,128)(2,1)}, bf16[4,4,128,256]{3,2,1,0:T(8,128)(2,1)}, u32[]{:S(2)}, u32[]{:S(2)}) collective-permute-start(bf16[4,4,128,256]{3,2,1,0:T(8,128)(2,1)} %get-tuple-element.16), channel_id=1, source_target_pairs={{0,4},{4,0},{1,5},{5,1},{2,6},{6,2},{3,7},{7,3},{8,12},{12,8},{9,1... | collective-permute-start | bytes 3145736 | tf_op jit(solution)/shard_map/ppermute | solution.py:270
  69.5 37.8 %all-to-all-start.1 = ((bf16[16,128,512]{2,1,0:T(8,128)(2,1)}), bf16[16,128,512]{2,1,0:T(8,128)(2,1)}, u32[]{:S(2)}, u32[]{:S(2)}) async-start(bf16[16,128,512]{2,1,0:T(8,128)(2,1)} %get-tuple-element.12), calls=%async_computation.1 | async-start | bytes 4194304 | tf_op jit(solution)/shard_map/all_to_all | solution.py:292
  107.2 37.0 %all-to-all-start.4 = ((bf16[128,16,512]{2,1,0:T(8,128)(2,1)}), bf16[128,16,512]{2,1,0:T(8,128)(2,1)}, u32[]{:S(2)}, u32[]{:S(2)}) async-start(bf16[128,16,512]{2,1,0:T(8,128)(2,1)} %bitcast.15), calls=%async_computation.4 | async-start | bytes 4194304 | tf_op jit(solution)/shard_map/all_to_all | solution.py:294
  144.2 36.1 %all-to-all-start.2 = ((bf16[128,16,512]{2,1,0:T(8,128)(2,1)}), bf16[128,16,512]{2,1,0:T(8,128)(2,1)S(1)}, u32[]{:S(2)}, u32[]{:S(2)}) async-start(bf16[128,16,512]{2,1,0:T(8,128)(2,1)} %bitcast.16), calls=%async_computation.2 | async-start | bytes 4194304 | tf_op jit(solution)/shard_map/all_to_all | solution.py:294
  180.4 1.3 copy-start.2

commit v3 on v2

--- a/solution.py
+++ b/solution.py
@@ -145,7 +145,7 @@
     lax.fori_loop(0, BLOCK // TILE, tile, 0)
 
 
-AHEAD = 3
+AHEAD = 8
 SPANS = (1, 2, 3, 4, 5, 7, 9)
 
 
@@ -183,7 +183,8 @@
 
 
 AXES = ("y", "z", "core", "x")
-CHUNKS = 2
+SIZES = (3, 5)
+FIRST = (0, 3)
 
 
 def pack_kernel(seat, tab, keys, values, out):
@@ -207,59 +208,47 @@
 
 def split_kernel(seat, tab, rows, *outs):
     cos, sin = tables(tab, seat[0])
-    count = 8 // len(outs)
     for g in range(4):
-        for j, out in enumerate(outs):
-            for h in range(count):
-                col = g * 1024 + (j * count + h) * 128
+        for first, size, out in zip(FIRST, SIZES, outs):
+            for h in range(size):
+                col = g * 1024 + (first + h) * 128
                 out[g, :, h * 128:h * 128 + 128] = rotated(rows[:, col:col + 128], cos, sin)
 
 
 def split(seat, tab, rows):
-    width = 1024 // CHUNKS
     return pl.pallas_call(
         split_kernel,
         grid=(4,),
-        out_shape=[jax.ShapeDtypeStruct((16, 128, width), jnp.bfloat16)] * CHUNKS,
+        out_shape=[jax.ShapeDtypeStruct((16, 128, n * 128), jnp.bfloat16) for n in SIZES],
         in_specs=[
             pl.BlockSpec(memory_space=pltpu.SMEM),
             pl.BlockSpec((512, 128), lambda g: (0, 0)),
             pl.BlockSpec((128, 4096), lambda g: (0, g)),
         ],
-        out_specs=[pl.BlockSpec((4, 128, width), lambda g: (g, 0, 0))] * CHUNKS,
+        out_specs=[pl.BlockSpec((4, 128, n * 128), lambda g: (g, 0, 0)) for n in SIZES],
         cost_estimate=pl.CostEstimate(flops=2 << 30, bytes_accessed=8 << 20, transcendentals=0),
         name="split",
     )(seat, tab, rows)
 
 
-def place_kernel(chunk, part, *refs):
-    out, sem = refs[-2:]
-    width = 1024 // CHUNKS
-    copies = []
-    for y in range(4):
-        for b in range(8):
+def place_kernel(*refs):
+    out = refs[-1]
+    for first, size, part in zip(FIRST, SIZES, refs[:-1]):
+        for b in range(4):
             for x in range(4):
-                copies.append(pltpu.make_async_copy(
-                    part.at[y, b, x],
-                    out.at[pl.ds(b * 16, 16), pl.ds((y * 4 + x) * 1024 + chunk * width, width)],
-                    sem.at[len(copies)]))
-    for c in copies:
-        c.start()
-    for c in copies:
-        c.wait()
-
-
-def place(chunk, part, rows):
-    before = [] if rows is None else [rows]
-    return pl.pallas_call(
-        functools.partial(place_kernel, chunk),
+                col = x * 1024 + first * 128
+                out[b * 16:b * 16 + 16, col:col + size * 128] = part[0, b, x]
+
+
+def place(parts):
+    return pl.pallas_call(
+        place_kernel,
+        grid=(4, 2),
         out_shape=jax.ShapeDtypeStruct((128, 16384), jnp.bfloat16),
-        in_specs=[pl.BlockSpec(memory_space=pltpu.VMEM)] + [pl.BlockSpec(memory_space=pl.ANY)] * len(before),
-        out_specs=pl.BlockSpec(memory_space=pl.ANY),
-        scratch_shapes=[pltpu.SemaphoreType.DMA((128,))],
-        input_output_aliases={1: 0} if before else {},
+        in_specs=[pl.BlockSpec((1, 4, 4, 16, n * 128), lambda y, b: (y, b, 0, 0, 0)) for n in SIZES],
+        out_specs=pl.BlockSpec((64, 4096), lambda y, b: (b, y)),
         name="place",
-    )(part, *before)
+    )(*parts)
 
 
 def ring(a, by):
@@ -284,16 +273,18 @@
     far_keys = ring(near[..., :128], 1)
     far_values = ring(left_values, -1)
     first = swap(jnp.where(core == 0, own, near))
-    third = swap(jnp.where(core == 0, near, jnp.concatenate([far_keys, far_values], axis=-1)))
+    parts[0] = lax.all_to_all(parts[0], ("y", "x"), split_axis=0, concat_axis=0, tiled=True)
+    parts[0], middle = lax.optimization_barrier((parts[0], near))
+    third = swap(jnp.where(core == 0, middle, jnp.concatenate([far_keys, far_values], axis=-1)))
     kv = (far_keys, far_values, third, near, first, own)
-    width = 1024 // CHUNKS
-    rows = None
-    for j, part in enumerate(parts):
-        part = lax.all_to_all(part, ("y", "x"), split_axis=0, concat_axis=0, tiled=True)
-        o = attend(8 // CHUNKS, doc_lengths, block_plan, at, part.reshape(4, 4, 128, width), kv)
-        o = lax.all_to_all(o.reshape(128, 16, width), AXES, split_axis=0, concat_axis=0, tiled=True)
-        rows = place(j, o.reshape(4, 8, 4, 16, width), rows)
-    return rows
+    done = []
+    for j, (size, part) in enumerate(zip(SIZES, parts)):
+        if j > 0:
+            part = lax.all_to_all(part, ("y", "x"), split_axis=0, concat_axis=0, tiled=True)
+        o = attend(size, doc_lengths, block_plan, at, part.reshape(4, 4, 128, size * 128), kv)
+        o = lax.all_to_all(o.reshape(128, 16, size * 128), AXES, split_axis=0, concat_axis=0, tiled=True)
+        done.append(o.reshape(4, 8, 4, 16, size * 128))
+    return place(done)
 
 
 def solution(mesh):

time: 186 us -> 190 us (1.022)
  blocking collectives: 0 us -> 50.4 us
  waiting for transfers between devices: 84.2 us -> 40.5 us
    all_to_all x0 -> x1, blocking collectives: none -> 50.4 us  [on_device(): lax.all_to_all(o.reshape(128, 16, size * 128), AXES, split_axis=0, concat...]
    all_to_all x2, waiting for transfers between devices: 37.3 us -> 0.81 us  [the longest x1 0.8 us: on_device(): lax.all_to_all(o.reshape(128, 16, size * 128), AXES, split_axis=0, concat...]
    ppermute x4, waiting for transfers between devices: 25 us -> 16.4 us  [ring(): return lax.ppermute(a, 'z', [(i, (i + by) % 4) for i in range(4)])]
    all_to_all x2 -> x1, starting transfers between devices: 10.3 us -> 4.47 us  [on_device(): lax.all_to_all(part, ('y', 'x'), split_axis=0, concat_axis=0, tiled=True)]
    ppermute x2, starting transfers between devices: 3.99 us -> 7.24 us  [swap(): return lax.ppermute(a, 'core', [(0, 1), (1, 0)])]
    ppermute x2, waiting for transfers between devices: 0.01 us -> 2.29 us  [swap(): return lax.ppermute(a, 'core', [(0, 1), (1, 0)])]
    all_to_all x2, starting transfers between devices: 11.4 us -> 13.6 us  [the longest x1 9.24 us: on_device(): lax.all_to_all(o.reshape(128, 16, size * 128), AXES, split_axis=0, concat...]
    pallas_call x2 -> x1, Pallas kernels: 8.02 us -> 6.67 us  [place(): pl.pallas_call(place_kernel, grid=(4, 2), out_shape=jax.ShapeDtypeStruct(...]
  transfers between devices with their start and end apart: 11 -> 10, of which waited for: 7 -> 7; matrix products, arithmetic and copies ran while one was open for 2% -> 1% of each run, Pallas kernels for 27% -> 24%
where the time goes in v3:
time: 190 us; the launch traced here: 191 us
  Pallas kernels  55.6 us (29%)
  blocking collectives  50.4 us (27%)
  waiting for transfers between devices  40.5 us (21%)
  starting transfers between devices  40 us (21%)
  local copies, waits for them, and re-layouts  3.23 us (2%)
    all_to_all x1, blocking collectives, on_device(): lax.all_to_all(o.reshape(128, 16, size * 128), AXES, split_axis=0, concat...  50.4 us
    pallas_call x2, Pallas kernels, attend(): pl.pallas_call(lambda *r: attn_kernel(heads, *r), out_shape=jax.ShapeDtyp...  40.9 us
    ppermute x4, waiting for transfers between devices, ring(): return lax.ppermute(a, 'z', [(i, (i + by) % 4) for i in range(4)])  16.4 us
    all_to_all x1, waiting for transfers between devices, on_device(): lax.all_to_all(part, ('y', 'x'), split_axis=0, concat_axis=0, tiled=True)  10.6 us
    all_to_all x1, waiting for transfers between devices, on_device(): lax.all_to_all(kv, ('y', 'x'), split_axis=0, concat_axis=0, tiled=True)  10.4 us
    all_to_all x1, starting transfers between devices, on_device(): lax.all_to_all(o.reshape(128, 16, size * 128), AXES, split_axis=0, concat...  9.24 us
    all_to_all x1, starting transfers between devices, on_device(): lax.all_to_all(kv, ('y', 'x'), split_axis=0, concat_axis=0, tiled=True)  7.57 us
    ppermute x2, starting transfers between devices, swap(): return lax.ppermute(a, 'core', [(0, 1), (1, 0)])  7.24 us
  transfers between devices with their start and end apart: 10, of which 7 were waited for; matrix products, arithmetic and copies ran while one was open for 1% of the time, Pallas kernels for 24%

profile of v3, /device:TPU:1, one launch (start us, length us, event | category | flops | bytes accessed | tf_op | source)
XLA Modules:
  0.0 191.1 jit_solution(2384876797529080485)
XLA Ops:
  0.0 2.3 %pack.1 = bf16[16,128,256]{2,1,0:T(8,128)(2,1)} custom-call(s32[1]{0:T(128)} %bitcast.1.seat, f32[512,128]{1,0:T(8,128)} %constant.26.clone.tab, bf16[128,1024]{1,0:T(8,128)(2,1)} %keys.1, bf16[128,1024]{1,0:T(8,128)(2,1)} %values.1), custom_call_target="tpu_custom_call" | custom-call | tf_op jit(solution)/shard_map/pack/pallas_call | solution.py:201
  2.3 7.6 %all-to-all-start = ((bf16[16,128,256]{2,1,0:T(8,128)(2,1)}), bf16[16,128,256]{2,1,0:T(8,128)(2,1)S(1)}, u32[]{:S(2)}, u32[]{:S(2)}) async-start(bf16[16,128,256]{2,1,0:T(8,128)(2,1)} %pack.1), calls=%async_computation | async-start | bytes 2097152 | tf_op jit(solution)/shard_map/all_to_all | solution.py:268
  9.9 5.7 %split.1 = (bf16[16,128,384]{2,1,0:T(8,128)(2,1)}, bf16[16,128,640]{2,1,0:T(8,128)(2,1)}) custom-call(s32[1]{0:T(128)} %bitcast.1.seat, f32[512,128]{1,0:T(8,128)} %constant.26.clone.tab, bf16[128,16384]{1,0:T(8,128)(2,1)} %rows.1), custom_call_target="tpu_custom_call" | custom-call | flops 2147483648 | bytes 8388608 | tf_op jit(solution)/shard_map/split/pallas_call | solution.py:219
  15.6 10.4 %all-to-all-done = bf16[16,128,256]{2,1,0:T(8,128)(2,1)S(1)} async-done(((bf16[16,128,256]{2,1,0:T(8,128)(2,1)}), bf16[16,128,256]{2,1,0:T(8,128)(2,1)S(1)}, u32[]{:S(2)}, u32[]{:S(2)}) %all-to-all-start) | async-done | bytes 1048608 | tf_op jit(solution)/shard_map/all_to_all | solution.py:268
  26.0 1.6 collective-permute-start
  27.6 4.4 %all-to-all-start.1 = ((bf16[16,128,384]{2,1,0:T(8,128)(2,1)}), bf16[16,128,384]{2,1,0:T(8,128)(2,1)}, u32[]{:S(2)}, u32[]{:S(2)}) async-start(bf16[16,128,384]{2,1,0:T(8,128)(2,1)} %get-tuple-element.14), calls=%async_computation.1 | async-start | bytes 3145728 | tf_op jit(solution)/shard_map/all_to_all | solution.py:276
  32.1 2.2 %collective-permute-start.2 = (bf16[4,4,128,128]{3,2,1,0:T(8,128)(2,1)S(1)}, bf16[4,4,128,128]{3,2,1,0:T(8,128)(2,1)}, u32[]{:S(2)}, u32[]{:S(2)}) collective-permute-start(bf16[4,4,128,128]{3,2,1,0:T(8,128)(2,1)S(1)} %slice.7), channel_id=1, source_target_pairs={{0,24},{8,0},{16,8},{24,16},{1,25},{9,1},{17,9},{25,17},{2,26},{10... | collective-permute-start | bytes 1572872 | tf_op jit(solution)/shard_map/ppermute | solution.py:255
  34.3 9.0 %collective-permute-done.2 = bf16[4,4,128,128]{3,2,1,0:T(8,128)(2,1)} collective-permute-done((bf16[4,4,128,128]{3,2,1,0:T(8,128)(2,1)S(1)}, bf16[4,4,128,128]{3,2,1,0:T(8,128)(2,1)}, u32[]{:S(2)}, u32[]{:S(2)}) %collective-permute-start.2) | collective-permute-done | bytes 524320 | tf_op jit(solution)/shard_map/ppermute | solution.py:255
  43.2 3.3 %collective-permute-start.3 = (bf16[4,4,128,128]{3,2,1,0:T(8,128)(2,1)}, bf16[4,4,128,128]{3,2,1,0:T(8,128)(2,1)S(1)}, u32[]{:S(2)}, u32[]{:S(2)}) collective-permute-start(bf16[4,4,128,128]{3,2,1,0:T(8,128)(2,1)} %collective-permute-done.2), channel_id=1, source_target_pairs={{0,24},{8,0},{16,8},{24,16},{1,25},{9,1},{17,9},{25,17},{2,26},{10... | collective-permute-start | bytes 1572872 | tf_op jit(solution)/shard_map/ppermute | solution.py:255
  46.5 4.3 %collective-permute-done.r_7_ = bf16[4,4,128,256]{3,2,1,0:T(8,128)(2,1)S(1)} collective-permute-done((bf16[4,4,128,256]{3,2,1,0:T(8,128)(2,1)S(1)}, bf16[4,4,128,256]{3,2,1,0:T(8,128)(2,1)S(1)}, u32[]{:S(2)}, u32[]{:S(2)}) %collective-permute-start) | collective-permute-done | bytes 1048608 | tf_op jit(solution)/shard_map/ppermute | solution.py:255
  51.7 1.1 broadcast_select_fusion
  52.8 3.1 %collective-permute-start.5 = (bf16[4,4,128,256]{3,2,1,0:T(8,128)(2,1)}, bf16[4,4,128,256]{3,2,1,0:T(8,128)(2,1)}, u32[]{:S(2)}, u32[]{:S(2)}) collective-permute-start(bf16[4,4,128,256]{3,2,1,0:T(8,128)(2,1)} %broadcast_select_fusion), channel_id=1, source_target_pairs={{0,4},{4,0},{1,5},{5,1},{2,6},{6,2},{3,7},{7,3},{8,12},{12,8},{9,1... | collective-permute-start | bytes 3145736 | tf_op jit(solution)/shard_map/ppermute | solution.py:259
  55.8 4.5 %all-to-all-start.3 = ((bf16[16,128,640]{2,1,0:T(8,128)(2,1)}), bf16[16,128,640]{2,1,0:T(8,128)(2,1)}, u32[]{:S(2)}, u32[]{:S(2)}) async-start(bf16[16,128,640]{2,1,0:T(8,128)(2,1)} %get-tuple-element.18), calls=%async_computation.3 | async-start | bytes 5242880 | tf_op jit(solution)/shard_map/all_to_all | solution.py:283
  60.3 3.2 %collective-permute-done.1.r_4_ = bf16[4,4,128,128]{3,2,1,0:T(8,128)(2,1)S(1)} collective-permute-done((bf16[4,4,128,128]{3,2,1,0:T(8,128)(2,1)}, bf16[4,4,128,128]{3,2,1,0:T(8,128)(2,1)S(1)}, u32[]{:S(2)}, u32[]{:S(2)}) %collective-permute-start.1) | collective-permute-done | bytes 524320 | tf_op jit(solution)/shard_map/ppermute | solution.py:255
  63.9 4.2 %collective-permute-start.4 = (bf16[4,4,128,256]{3,2,1,0:T(8,128)(2,1)S(1)}, bf16[4,4,128,256]{3,2,1,0:T(8,128)(2,1)S(1)}, u32[]{:S(2)}, u32[]{:S(2)}) collective-permute-start(bf16[4,4,128,256]{3,2,1,0:T(8,128)(2,1)S(1)} %maximum_select_fusion), channel_id=1, source_target_pairs={{0,4},{4,0},{1,5},{5,1},{2,6},{6,2},{3,7},{7,3},{8,12},{12,8},{9,1... | collective-permute-start | bytes 3145736 | tf_op jit(solution)/shard_map/ppermute | solution.py:259
  68.0 2.3 %collective-permute-done.4.r_6_ = bf16[4,4,128,256]{3,2,1,0:T(8,128)(2,1)S(1)} collective-permute-done((bf16[4,4,128,256]{3,2,1,0:T(8,128)(2,1)S(1)}, bf16[4,4,128,256]{3,2,1,0:T(8,128)(2,1)S(1)}, u32[]{:S(2)}, u32[]{:S(2)}) %collective-permute-start.4) | collective-permute-done | bytes 1048608 | tf_op jit(solution)/shard_map/ppermute | solution.py:259
  70.3 17.9 %attend.2 = bf16[32,4,16,384]{3,2,1,0:T(8,128)(2,1)} custom-call(s32[16]{0:T(128)S(1)} %copy-done.3, s32[32,32]{1,0:T(8,128)S(1)} %copy-done.2, s32[1]{0:T(128)} %bitcast.r_2_, bf16[4,4,128,384]{3,2,1,0:T(8,128)(2,1)} %bitcast.3.r_3_, bf16[4,4,128,128]{3,2,1,0:T(8,128)(2,1)S(1)} %collective-permute-done.1.r_4_, ...), custom_call_target="tpu_custom_call" | custom-call | flops 14495514624 | bytes 16777216 | tf_op jit(solution)/shard_map/attend/pallas_call | solution.py:162
  88.2 1.0 copy-done
  89.2 10.6 %all-to-all-done.3 = bf16[16,128,640]{2,1,0:T(8,128)(2,1)} async-done(((bf16[16,128,640]{2,1,0:T(8,128)(2,1)}), bf16[16,128,640]{2,1,0:T(8,128)(2,1)}, u32[]{:S(2)}, u32[]{:S(2)}) %all-to-all-start.3) | async-done | bytes 2621472 | tf_op jit(solution)/shard_map/all_to_all | solution.py:283
  99.8 9.2 %all-to-all-start.2 = ((bf16[128,16,384]{2,1,0:T(8,128)(2,1)}), bf16[128,16,384]{2,1,0:T(8,128)(2,1)}, u32[]{:S(2)}, u32[]{:S(2)}) async-start(bf16[128,16,384]{2,1,0:T(8,128)(2,1)} %bitcast.16), calls=%async_computation.2 | async-start | bytes 3145728 | tf_op jit(solution)/shard_map/all_to_all | solution.py:285
  109.0 1.2 copy-done.1
  110.3 23.0 %attend.3 = bf16[32,4,16,640]{3,2,1,0:T(8,128)(2,1)} custom-call(s32[16]{0:T(128)S(1)} %copy-done.3, s32[32,32]{1,0:T(8,128)S(1)} %copy-done.2, s32[1]{0:T(128)} %bitcast.r_2_, bf16[4,4,128,640]{3,2,1,0:T(8,128)(2,1)} %bitcast.6.r_3_, bf16[4,4,128,128]{3,2,1,0:T(8,128)(2,1)S(1)} %collective-permute-done.1.r_4_, ...), custom_call_target="tpu_custom_call" | custom-call | flops 24159191040 | bytes 16777216 | tf_op jit(solution)/shard_map/attend/pallas_call | solution.py:162
  134.1 50.4 %all_to_all.25 = bf16[128,16,640]{2,1,0:T(8,128)(2,1)} all-to-all(bf16[128,16,640]{2,1,0:T(8,128)(2,1)} %bitcast.15), channel_id=1, replica_groups=mesh['y'=4,'z'=4,'core'=2,'x'=4] {'y','z','core','x'}, dimensions={0} | all-to-all | bytes 5242880 | tf_op jit(solution)/shard_map/all_to_all | solution.py:285
  184.4 6.7 %place.1 = bf16[128,16384]{1,0:T(8,128)(2,1)} custom-call(bf16[4,8,4,16,384]{4,3,2,1,0:T(8,128)(2,1)} %bitcast.5.refs_0_, bf16[4,8,4,16,640]{4,3,2,1,0:T(8,128)(2,1)} %bitcast.14), custom_call_target="tpu_custom_call" | custom-call | tf_op jit(solution)/shard_map/place/pallas_call | solution.py:244
  (14 shorter events, 2.2 us)
Async XLA Ops:
  2.3 23.6 %all-to-all-start = ((bf16[16,128,256]{2,1,0:T(8,128)(2,1)}), bf16[16,128,256]{2,1,0:T(8,128)(2,1)S(1)}, u32[]{:S(2)}, u32[]{:S(2)}) async-start(bf16[16,128,256]{2,1,0:T(8,128)(2,1)} %pack.1), calls=%async_computation | async-start | bytes 2097152 | tf_op jit(solution)/shard_map/all_to_all | solution.py:268
  26.0 24.8 %collective-permute-start = (bf16[4,4,128,256]{3,2,1,0:T(8,128)(2,1)S(1)}, bf16[4,4,128,256]{3,2,1,0:T(8,128)(2,1)S(1)}, u32[]{:S(2)}, u32[]{:S(2)}) collective-permute-start(bf16[4,4,128,256]{3,2,1,0:T(8,128)(2,1)S(1)} %bitcast.9), channel_id=1, source_target_pairs={{0,8},{8,16},{16,24},{24,0},{1,9},{9,17},{17,25},{25,1},{2,10},{10... | collective-permute-start | bytes 3145736 | tf_op jit(solution)/shard_map/ppermute | solution.py:255
  27.6 28.2 %all-to-all-start.1 = ((bf16[16,128,384]{2,1,0:T(8,128)(2,1)}), bf16[16,128,384]{2,1,0:T(8,128)(2,1)}, u32[]{:S(2)}, u32[]{:S(2)}) async-start(bf16[16,128,384]{2,1,0:T(8,128)(2,1)} %get-tuple-element.14), calls=%async_computation.1 | async-start | bytes 3145728 | tf_op jit(solution)/shard_map/all_to_all | solution.py:276
  32.1 11.1 %collective-permute-start.2 = (bf16[4,4,128,128]{3,2,1,0:T(8,128)(2,1)S(1)}, bf16[4,4,128,128]{3,2,1,0:T(8,128)(2,1)}, u32[]{:S(2)}, u32[]{:S(2)}) collective-permute-start(bf16[4,4,128,128]{3,2,1,0:T(8,128)(2,1)S(1)} %slice.7), channel_id=1, source_target_pairs={{0,24},{8,0},{16,8},{24,16},{1,25},{9,1},{17,9},{25,17},{2,26},{10... | collective-permute-start | bytes 1572872 | tf_op jit(solution)/shard_map/ppermute | solution.py:255
  43.2 17.1 %collective-permute-start.3 = (bf16[4,4,128,128]{3,2,1,0:T(8,128)(2,1)}, bf16[4,4,128,128]{3,2,1,0:T(8,128)(2,1)S(1)}, u32[]{:S(2)}, u32[]{:S(2)}) collective-permute-start(bf16[4,4,128,128]{3,2,1,0:T(8,128)(2,1)} %collective-permute-done.2), channel_id=1, source_target_pairs={{0,24},{8,0},{16,8},{24,16},{1,25},{9,1},{17,9},{25,17},{2,26},{10... | collective-permute-start | bytes 1572872 | tf_op jit(solution)/shard_map/ppermute | solution.py:255
  51.7 11.8 %collective-permute-start.1 = (bf16[4,4,128,128]{3,2,1,0:T(8,128)(2,1)}, bf16[4,4,128,128]{3,2,1,0:T(8,128)(2,1)S(1)}, u32[]{:S(2)}, u32[]{:S(2)}) collective-permute-start(bf16[4,4,128,128]{3,2,1,0:T(8,128)(2,1)} %slice.8), channel_id=1, source_target_pairs={{0,8},{8,16},{16,24},{24,0},{1,9},{9,17},{17,25},{25,1},{2,10},{10... | collective-permute-start | bytes 1572872 | tf_op jit(solution)/shard_map/ppermute | solution.py:255
  52.8 15.3 %collective-permute-start.5 = (bf16[4,4,128,256]{3,2,1,0:T(8,128)(2,1)}, bf16[4,4,128,256]{3,2,1,0:T(8,128)(2,1)}, u32[]{:S(2)}, u32[]{:S(2)}) collective-permute-start(bf16[4,4,128,256]{3,2,1,0:T(8,128)(2,1)} %broadcast_select_fusion), channel_id=1, source_target_pairs={{0,4},{4,0},{1,5},{5,1},{2,6},{6,2},{3,7},{7,3},{8,12},{12,8},{9,1... | collective-permute-start | bytes 3145736 | tf_op jit(solution)/shard_map/ppermute | solution.py:259
  55.8 43.9 %all-to-all-start.3 = ((bf16[16,128,640]{2,1,0:T(8,128)(2,1)}), bf16[16,128,640]{2,1,0:T(8,128)(2,1)}, u32[]{:S(2)}, u32[]{:S(2)}) async-start(bf16[16,128,640]{2,1,0:T(8,128)(2,1)} %get-tuple-element.18), calls=%async_computation.3 | async-start | bytes 5242880 | tf_op jit(solution)/shard_map/all_to_all | solution.py:283
  60.3 10.0 %copy-start.2 = (s32[32,32]{1,0:T(8,128)S(1)}, s32[32,32]{1,0:T(8,128)}, u32[]{:S(2)}) copy-start(s32[32,32]{1,0:T(8,128)} %r_1_.3) | copy-start | bytes 12292
  60.3 10.0 %copy-start.3 = (s32[16]{0:T(128)S(1)}, s32[16]{0:T(128)}, u32[]{:S(2)}) copy-start(s32[16]{0:T(128)} %r_0_.3) | copy-start | bytes 196
  63.9 6.5 %collective-permute-start.4 = (bf16[4,4,128,256]{3,2,1,0:T(8,128)(2,1)S(1)}, bf16[4,4,128,256]{3,2,1,0:T(8,128)(2,1)S(1)}, u32[]{:S(2)}, u32[]{:S(2)}) collective-permute-start(bf16[4,4,128,256]{3,2,1,0:T(8,128)(2,1)S(1)} %maximum_select_fusion), channel_id=1, source_target_pairs={{0,4},{4,0},{1,5},{5,1},{2,6},{6,2},{3,7},{7,3},{8,12},{12,8},{9,1... | collective-permute-start | bytes 3145736 | tf_op jit(solution)/shard_map/ppermute | solution.py:259
  88.2 1.0 copy-start
  99.8 34.3 %all-to-all-start.2 = ((bf16[128,16,384]{2,1,0:T(8,128)(2,1)}), bf16[128,16,384]{2,1,0:T(8,128)(2,1)}, u32[]{:S(2)}, u32[]{:S(2)}) async-start(bf16[128,16,384]{2,1,0:T(8,128)(2,1)} %bitcast.16), calls=%async_computation.2 | async-start | bytes 3145728 | tf_op jit(solution)/shard_map/all_to_all | solution.py:285
  109.0 1.2 copy-start.1

commit v4 on v3

--- a/solution.py
+++ b/solution.py
@@ -64,11 +64,9 @@
         begin = end
     starts = jnp.where(lane == NDOC, -(1 << 20), starts)
 
-    def note(r, c):
+    for r in range(32):
         inv[plan_ref[s, r]] = r
-        return c
-
-    lax.fori_loop(0, 32, note, 0)
+
     def inside(pos):
         p = pos + lax.broadcasted_iota(jnp.int32, (128, 128), 0)
         return (p >= starts) & (p < ends)
@@ -183,8 +181,8 @@
 
 
 AXES = ("y", "z", "core", "x")
-SIZES = (3, 5)
-FIRST = (0, 3)
+SIZES = (4, 4)
+FIRST = (0, 4)
 
 
 def pack_kernel(seat, tab, keys, values, out):
@@ -234,7 +232,7 @@
 def place_kernel(*refs):
     out = refs[-1]
     for first, size, part in zip(FIRST, SIZES, refs[:-1]):
-        for b in range(4):
+        for b in range(8):
             for x in range(4):
                 col = x * 1024 + first * 128
                 out[b * 16:b * 16 + 16, col:col + size * 128] = part[0, b, x]
@@ -243,10 +241,10 @@
 def place(parts):
     return pl.pallas_call(
         place_kernel,
-        grid=(4, 2),
+        grid=(4,),
         out_shape=jax.ShapeDtypeStruct((128, 16384), jnp.bfloat16),
-        in_specs=[pl.BlockSpec((1, 4, 4, 16, n * 128), lambda y, b: (y, b, 0, 0, 0)) for n in SIZES],
-        out_specs=pl.BlockSpec((64, 4096), lambda y, b: (b, y)),
+        in_specs=[pl.BlockSpec((1, 8, 4, 16, n * 128), lambda y: (y, 0, 0, 0, 0)) for n in SIZES],
+        out_specs=pl.BlockSpec((128, 4096), lambda y: (0, y)),
         name="place",
     )(*parts)
 
@@ -275,7 +273,8 @@
     first = swap(jnp.where(core == 0, own, near))
     parts[0] = lax.all_to_all(parts[0], ("y", "x"), split_axis=0, concat_axis=0, tiled=True)
     parts[0], middle = lax.optimization_barrier((parts[0], near))
-    third = swap(jnp.where(core == 0, middle, jnp.concatenate([far_keys, far_values], axis=-1)))
+    third = jnp.where(core == 0, middle, jnp.concatenate([far_keys, far_values], axis=-1))
+    third = swap(third)
     kv = (far_keys, far_values, third, near, first, own)
     done = []
     for j, (size, part) in enumerate(zip(SIZES, parts)):
@@ -290,6 +289,5 @@
 def solution(mesh):
     fine = jax.sharding.Mesh(mesh.devices.reshape(4, 4, 2, 4), AXES)
     rows = P(AXES, None)
-    return jax.shard_map(
-        on_device, mesh=fine, in_specs=(rows, rows, rows, P(), P()), out_specs=rows, check_vma=False
-    )
+
+    return jax.shard_map(on_device, mesh=fine, in_specs=(rows, rows, rows, P(), P()), out_specs=rows, check_vma=False)

time: 190 us -> 198 us (1.042); the launches traced: 191 us -> 197 us
  waiting for transfers between devices: 40.5 us -> 57.7 us
  blocking collectives: 50.4 us -> 35.6 us
  starting transfers between devices: 40 us -> 50.5 us
  Pallas kernels: 55.6 us -> 49.7 us
  local copies, waits for them, and re-layouts: 3.23 us -> 0.99 us
    all_to_all x1, waiting for transfers between devices: 0.01 us -> 21.6 us  [on_device(): lax.all_to_all(parts[0], ('y', 'x'), split_axis=0, concat_axis=0, tiled=T...]
    all_to_all x1, blocking collectives: 50.4 us -> 35.6 us  [on_device(): lax.all_to_all(o.reshape(128, 16, size * 128), AXES, split_axis=0, concat...]
    all_to_all x1, waiting for transfers between devices: 0.8 us -> 12.2 us  [on_device(): lax.all_to_all(o.reshape(128, 16, size * 128), AXES, split_axis=0, concat...]
    all_to_all x1, starting transfers between devices: 9.24 us -> 17 us  [on_device(): lax.all_to_all(o.reshape(128, 16, size * 128), AXES, split_axis=0, concat...]
    ppermute x4, waiting for transfers between devices: 16.4 us -> 8.75 us  [ring(): return lax.ppermute(a, 'z', [(i, (i + by) % 4) for i in range(4)])]
    all_to_all x1, waiting for transfers between devices: 10.6 us -> 4.82 us  [on_device(): lax.all_to_all(part, ('y', 'x'), split_axis=0, concat_axis=0, tiled=True)]
    pallas_call x2, Pallas kernels: 40.9 us -> 37 us  [attend(): pl.pallas_call(lambda *r: attn_kernel(heads, *r), out_shape=jax.ShapeDtyp...]
    all_to_all x1, starting transfers between devices: 4.47 us -> 7.83 us  [on_device(): lax.all_to_all(part, ('y', 'x'), split_axis=0, concat_axis=0, tiled=True)]
  transfers between devices with their start and end apart: 10 -> 10, of which waited for: 7 -> 6; matrix products, arithmetic and copies ran while one was open for 1% -> 2% of each run, Pallas kernels for 24% -> 12%
where the time goes in v4:
time: 198 us; the launch traced here: 197 us
  waiting for transfers between devices  57.7 us (29%)
  starting transfers between devices  50.5 us (26%)
  Pallas kernels  49.7 us (25%)
  blocking collectives  35.6 us (18%)
  other arithmetic  2.41 us (1%)
    pallas_call x2, Pallas kernels, attend(): pl.pallas_call(lambda *r: attn_kernel(heads, *r), out_shape=jax.ShapeDtyp...  37 us
    all_to_all x1, blocking collectives, on_device(): lax.all_to_all(o.reshape(128, 16, size * 128), AXES, split_axis=0, concat...  35.6 us
    all_to_all x1, waiting for transfers between devices, on_device(): lax.all_to_all(parts[0], ('y', 'x'), split_axis=0, concat_axis=0, tiled=T...  21.6 us
    all_to_all x1, starting transfers between devices, on_device(): lax.all_to_all(o.reshape(128, 16, size * 128), AXES, split_axis=0, concat...  17 us
    all_to_all x1, waiting for transfers between devices, on_device(): lax.all_to_all(o.reshape(128, 16, size * 128), AXES, split_axis=0, concat...  12.2 us
    all_to_all x1, waiting for transfers between devices, on_device(): lax.all_to_all(kv, ('y', 'x'), split_axis=0, concat_axis=0, tiled=True)  10.3 us
    ppermute x4, waiting for transfers between devices, ring(): return lax.ppermute(a, 'z', [(i, (i + by) % 4) for i in range(4)])  8.75 us
    all_to_all x1, starting transfers between devices, on_device(): lax.all_to_all(part, ('y', 'x'), split_axis=0, concat_axis=0, tiled=True)  7.83 us
  transfers between devices with their start and end apart: 10, of which 6 were waited for; matrix products, arithmetic and copies ran while one was open for 2% of the time, Pallas kernels for 12%

profile of v4, /device:TPU:1, one launch (start us, length us, event | category | flops | bytes accessed | tf_op | source)
XLA Modules:
  0.0 197.0 jit_solution(16625112120970514474)
XLA Ops:
  0.0 2.3 %pack.1 = bf16[16,128,256]{2,1,0:T(8,128)(2,1)} custom-call(s32[1]{0:T(128)} %bitcast.1.seat, f32[512,128]{1,0:T(8,128)} %constant.26.clone.tab, bf16[128,1024]{1,0:T(8,128)(2,1)} %keys.1, bf16[128,1024]{1,0:T(8,128)(2,1)} %values.1), custom_call_target="tpu_custom_call" | custom-call | tf_op jit(solution)/shard_map/pack/pallas_call | solution.py:199
  2.3 7.6 %all-to-all-start = ((bf16[16,128,256]{2,1,0:T(8,128)(2,1)}), bf16[16,128,256]{2,1,0:T(8,128)(2,1)S(1)}, u32[]{:S(2)}, u32[]{:S(2)}) async-start(bf16[16,128,256]{2,1,0:T(8,128)(2,1)} %pack.1), calls=%async_computation | async-start | bytes 2097152 | tf_op jit(solution)/shard_map/all_to_all | solution.py:266
  9.9 5.7 %split.1 = (bf16[16,128,512]{2,1,0:T(8,128)(2,1)}, bf16[16,128,512]{2,1,0:T(8,128)(2,1)}) custom-call(s32[1]{0:T(128)} %bitcast.1.seat, f32[512,128]{1,0:T(8,128)} %constant.26.clone.tab, bf16[128,16384]{1,0:T(8,128)(2,1)} %rows.1), custom_call_target="tpu_custom_call" | custom-call | flops 2147483648 | bytes 8388608 | tf_op jit(solution)/shard_map/split/pallas_call | solution.py:217
  15.6 10.3 %all-to-all-done = bf16[16,128,256]{2,1,0:T(8,128)(2,1)S(1)} async-done(((bf16[16,128,256]{2,1,0:T(8,128)(2,1)}), bf16[16,128,256]{2,1,0:T(8,128)(2,1)S(1)}, u32[]{:S(2)}, u32[]{:S(2)}) %all-to-all-start) | async-done | bytes 1048608 | tf_op jit(solution)/shard_map/all_to_all | solution.py:266
  25.9 4.4 %all-to-all-start.1 = ((bf16[16,128,512]{2,1,0:T(8,128)(2,1)}), bf16[16,128,512]{2,1,0:T(8,128)(2,1)}, u32[]{:S(2)}, u32[]{:S(2)}) async-start(bf16[16,128,512]{2,1,0:T(8,128)(2,1)} %get-tuple-element.14), calls=%async_computation.1 | async-start | bytes 4194304 | tf_op jit(solution)/shard_map/all_to_all | solution.py:274
  30.4 1.7 collective-permute-start
  32.2 2.2 %collective-permute-start.2 = (bf16[4,4,128,128]{3,2,1,0:T(8,128)(2,1)S(1)}, bf16[4,4,128,128]{3,2,1,0:T(8,128)(2,1)}, u32[]{:S(2)}, u32[]{:S(2)}) collective-permute-start(bf16[4,4,128,128]{3,2,1,0:T(8,128)(2,1)S(1)} %slice.7), channel_id=1, source_target_pairs={{0,24},{8,0},{16,8},{24,16},{1,25},{9,1},{17,9},{25,17},{2,26},{10... | collective-permute-start | bytes 1572872 | tf_op jit(solution)/shard_map/ppermute | solution.py:253
  34.4 21.6 %all-to-all-done.1 = bf16[16,128,512]{2,1,0:T(8,128)(2,1)} async-done(((bf16[16,128,512]{2,1,0:T(8,128)(2,1)}), bf16[16,128,512]{2,1,0:T(8,128)(2,1)}, u32[]{:S(2)}, u32[]{:S(2)}) %all-to-all-start.1) | async-done | bytes 2097184 | tf_op jit(solution)/shard_map/all_to_all | solution.py:274
  56.0 7.8 %all-to-all-start.3 = ((bf16[16,128,512]{2,1,0:T(8,128)(2,1)}), bf16[16,128,512]{2,1,0:T(8,128)(2,1)}, u32[]{:S(2)}, u32[]{:S(2)}) async-start(bf16[16,128,512]{2,1,0:T(8,128)(2,1)} %get-tuple-element.18), calls=%async_computation.3 | async-start | bytes 4194304 | tf_op jit(solution)/shard_map/all_to_all | solution.py:282
  63.9 3.8 %collective-permute-start.3 = (bf16[4,4,128,128]{3,2,1,0:T(8,128)(2,1)}, bf16[4,4,128,128]{3,2,1,0:T(8,128)(2,1)S(1)}, u32[]{:S(2)}, u32[]{:S(2)}) collective-permute-start(bf16[4,4,128,128]{3,2,1,0:T(8,128)(2,1)} %collective-permute-done.2), channel_id=1, source_target_pairs={{0,24},{8,0},{16,8},{24,16},{1,25},{9,1},{17,9},{25,17},{2,26},{10... | collective-permute-start | bytes 1572872 | tf_op jit(solution)/shard_map/ppermute | solution.py:253
  67.7 0.9 slice.8
  68.6 1.1 broadcast_select_fusion
  69.7 2.6 %collective-permute-start.5 = (bf16[4,4,128,256]{3,2,1,0:T(8,128)(2,1)}, bf16[4,4,128,256]{3,2,1,0:T(8,128)(2,1)}, u32[]{:S(2)}, u32[]{:S(2)}) collective-permute-start(bf16[4,4,128,256]{3,2,1,0:T(8,128)(2,1)} %broadcast_select_fusion), channel_id=1, source_target_pairs={{0,4},{4,0},{1,5},{5,1},{2,6},{6,2},{3,7},{7,3},{8,12},{12,8},{9,1... | collective-permute-start | bytes 3145736 | tf_op jit(solution)/shard_map/ppermute | solution.py:257
  72.3 4.7 %collective-permute-done.3.r_5_ = bf16[4,4,128,128]{3,2,1,0:T(8,128)(2,1)S(1)} collective-permute-done((bf16[4,4,128,128]{3,2,1,0:T(8,128)(2,1)}, bf16[4,4,128,128]{3,2,1,0:T(8,128)(2,1)S(1)}, u32[]{:S(2)}, u32[]{:S(2)}) %collective-permute-start.3) | collective-permute-done | bytes 524320 | tf_op jit(solution)/shard_map/ppermute | solution.py:253
  77.0 4.0 %collective-permute-done.1.r_4_ = bf16[4,4,128,128]{3,2,1,0:T(8,128)(2,1)S(1)} collective-permute-done((bf16[4,4,128,128]{3,2,1,0:T(8,128)(2,1)}, bf16[4,4,128,128]{3,2,1,0:T(8,128)(2,1)S(1)}, u32[]{:S(2)}, u32[]{:S(2)}) %collective-permute-start.1) | collective-permute-done | bytes 524320 | tf_op jit(solution)/shard_map/ppermute | solution.py:253
  81.0 1.3 maximum_select_fusion
  82.3 3.3 %collective-permute-start.4 = (bf16[4,4,128,256]{3,2,1,0:T(8,128)(2,1)}, bf16[4,4,128,256]{3,2,1,0:T(8,128)(2,1)}, u32[]{:S(2)}, u32[]{:S(2)}) collective-permute-start(bf16[4,4,128,256]{3,2,1,0:T(8,128)(2,1)} %maximum_select_fusion), channel_id=1, source_target_pairs={{0,4},{4,0},{1,5},{5,1},{2,6},{6,2},{3,7},{7,3},{8,12},{12,8},{9,1... | collective-permute-start | bytes 3145736 | tf_op jit(solution)/shard_map/ppermute | solution.py:257
  85.7 4.8 %all-to-all-done.3 = bf16[16,128,512]{2,1,0:T(8,128)(2,1)} async-done(((bf16[16,128,512]{2,1,0:T(8,128)(2,1)}), bf16[16,128,512]{2,1,0:T(8,128)(2,1)}, u32[]{:S(2)}, u32[]{:S(2)}) %all-to-all-start.3) | async-done | bytes 2097184 | tf_op jit(solution)/shard_map/all_to_all | solution.py:282
  90.5 18.5 %attend.3 = bf16[32,4,16,512]{3,2,1,0:T(8,128)(2,1)} custom-call(s32[16]{0:T(128)S(1)} %copy-done.1, s32[32,32]{1,0:T(8,128)S(1)} %copy-done, s32[1]{0:T(128)} %bitcast.r_2_, bf16[4,4,128,512]{3,2,1,0:T(8,128)(2,1)} %bitcast.6.r_3_, bf16[4,4,128,128]{3,2,1,0:T(8,128)(2,1)S(1)} %collective-permute-done.1.r_4_, ...), custom_call_target="tpu_custom_call" | custom-call | flops 19327352832 | bytes 16777216 | tf_op jit(solution)/shard_map/attend/pallas_call | solution.py:160
  109.1 17.0 %all-to-all-start.4 = ((bf16[128,16,512]{2,1,0:T(8,128)(2,1)}), bf16[128,16,512]{2,1,0:T(8,128)(2,1)}, u32[]{:S(2)}, u32[]{:S(2)}) async-start(bf16[128,16,512]{2,1,0:T(8,128)(2,1)} %bitcast.15), calls=%async_computation.4 | async-start | bytes 4194304 | tf_op jit(solution)/shard_map/all_to_all | solution.py:284
  126.1 18.4 %attend.2 = bf16[32,4,16,512]{3,2,1,0:T(8,128)(2,1)} custom-call(s32[16]{0:T(128)S(1)} %copy-done.1, s32[32,32]{1,0:T(8,128)S(1)} %copy-done, s32[1]{0:T(128)} %bitcast.r_2_, bf16[4,4,128,512]{3,2,1,0:T(8,128)(2,1)} %bitcast.3.r_3_, bf16[4,4,128,128]{3,2,1,0:T(8,128)(2,1)S(1)} %collective-permute-done.1.r_4_, ...), custom_call_target="tpu_custom_call" | custom-call | flops 19327352832 | bytes 16777216 | tf_op jit(solution)/shard_map/attend/pallas_call | solution.py:160
  144.5 12.2 %all-to-all-done.4 = bf16[128,16,512]{2,1,0:T(8,128)(2,1)} async-done(((bf16[128,16,512]{2,1,0:T(8,128)(2,1)}), bf16[128,16,512]{2,1,0:T(8,128)(2,1)}, u32[]{:S(2)}, u32[]{:S(2)}) %all-to-all-start.4) | async-done | bytes 2097184 | tf_op jit(solution)/shard_map/all_to_all | solution.py:284
  156.7 35.6 %all_to_all.25 = bf16[128,16,512]{2,1,0:T(8,128)(2,1)} all-to-all(bf16[128,16,512]{2,1,0:T(8,128)(2,1)} %bitcast.16), channel_id=1, replica_groups=mesh['y'=4,'z'=4,'core'=2,'x'=4] {'y','z','core','x'}, dimensions={0} | all-to-all | bytes 4194304 | tf_op jit(solution)/shard_map/all_to_all | solution.py:284
  192.3 4.7 %place.1 = bf16[128,16384]{1,0:T(8,128)(2,1)} custom-call(bf16[4,8,4,16,512]{4,3,2,1,0:T(8,128)(2,1)} %bitcast.14, bf16[4,8,4,16,512]{4,3,2,1,0:T(8,128)(2,1)} %bitcast.8.refs_1_), custom_call_target="tpu_custom_call" | custom-call | tf_op jit(solution)/shard_map/place/pallas_call | solution.py:242
  (10 shorter events, 0.1 us)
Async XLA Ops:
  2.3 23.6 %all-to-all-start = ((bf16[16,128,256]{2,1,0:T(8,128)(2,1)}), bf16[16,128,256]{2,1,0:T(8,128)(2,1)S(1)}, u32[]{:S(2)}, u32[]{:S(2)}) async-start(bf16[16,128,256]{2,1,0:T(8,128)(2,1)} %pack.1), calls=%async_computation | async-start | bytes 2097152 | tf_op jit(solution)/shard_map/all_to_all | solution.py:266
  25.9 30.1 %all-to-all-start.1 = ((bf16[16,128,512]{2,1,0:T(8,128)(2,1)}), bf16[16,128,512]{2,1,0:T(8,128)(2,1)}, u32[]{:S(2)}, u32[]{:S(2)}) async-start(bf16[16,128,512]{2,1,0:T(8,128)(2,1)} %get-tuple-element.14), calls=%async_computation.1 | async-start | bytes 4194304 | tf_op jit(solution)/shard_map/all_to_all | solution.py:274
  30.4 37.3 %collective-permute-start = (bf16[4,4,128,256]{3,2,1,0:T(8,128)(2,1)S(1)}, bf16[4,4,128,256]{3,2,1,0:T(8,128)(2,1)S(1)}, u32[]{:S(2)}, u32[]{:S(2)}) collective-permute-start(bf16[4,4,128,256]{3,2,1,0:T(8,128)(2,1)S(1)} %bitcast.9), channel_id=1, source_target_pairs={{0,8},{8,16},{16,24},{24,0},{1,9},{9,17},{17,25},{25,1},{2,10},{10... | collective-permute-start | bytes 3145736 | tf_op jit(solution)/shard_map/ppermute | solution.py:253
  32.2 31.7 %collective-permute-start.2 = (bf16[4,4,128,128]{3,2,1,0:T(8,128)(2,1)S(1)}, bf16[4,4,128,128]{3,2,1,0:T(8,128)(2,1)}, u32[]{:S(2)}, u32[]{:S(2)}) collective-permute-start(bf16[4,4,128,128]{3,2,1,0:T(8,128)(2,1)S(1)} %slice.7), channel_id=1, source_target_pairs={{0,24},{8,0},{16,8},{24,16},{1,25},{9,1},{17,9},{25,17},{2,26},{10... | collective-permute-start | bytes 1572872 | tf_op jit(solution)/shard_map/ppermute | solution.py:253
  56.0 34.5 %all-to-all-start.3 = ((bf16[16,128,512]{2,1,0:T(8,128)(2,1)}), bf16[16,128,512]{2,1,0:T(8,128)(2,1)}, u32[]{:S(2)}, u32[]{:S(2)}) async-start(bf16[16,128,512]{2,1,0:T(8,128)(2,1)} %get-tuple-element.18), calls=%async_computation.3 | async-start | bytes 4194304 | tf_op jit(solution)/shard_map/all_to_all | solution.py:282
  63.9 13.1 %collective-permute-start.3 = (bf16[4,4,128,128]{3,2,1,0:T(8,128)(2,1)}, bf16[4,4,128,128]{3,2,1,0:T(8,128)(2,1)S(1)}, u32[]{:S(2)}, u32[]{:S(2)}) collective-permute-start(bf16[4,4,128,128]{3,2,1,0:T(8,128)(2,1)} %collective-permute-done.2), channel_id=1, source_target_pairs={{0,24},{8,0},{16,8},{24,16},{1,25},{9,1},{17,9},{25,17},{2,26},{10... | collective-permute-start | bytes 1572872 | tf_op jit(solution)/shard_map/ppermute | solution.py:253
  68.6 12.4 %collective-permute-start.1 = (bf16[4,4,128,128]{3,2,1,0:T(8,128)(2,1)}, bf16[4,4,128,128]{3,2,1,0:T(8,128)(2,1)S(1)}, u32[]{:S(2)}, u32[]{:S(2)}) collective-permute-start(bf16[4,4,128,128]{3,2,1,0:T(8,128)(2,1)} %slice.8), channel_id=1, source_target_pairs={{0,8},{8,16},{16,24},{24,0},{1,9},{9,17},{17,25},{25,1},{2,10},{10... | collective-permute-start | bytes 1572872 | tf_op jit(solution)/shard_map/ppermute | solution.py:253
  69.7 20.8 %copy-start = (s32[32,32]{1,0:T(8,128)S(1)}, s32[32,32]{1,0:T(8,128)}, u32[]{:S(2)}) copy-start(s32[32,32]{1,0:T(8,128)} %r_1_.3) | copy-start | bytes 12292
  69.7 20.8 %copy-start.1 = (s32[16]{0:T(128)S(1)}, s32[16]{0:T(128)}, u32[]{:S(2)}) copy-start(s32[16]{0:T(128)} %r_0_.3) | copy-start | bytes 196
  69.7 20.8 %collective-permute-start.5 = (bf16[4,4,128,256]{3,2,1,0:T(8,128)(2,1)}, bf16[4,4,128,256]{3,2,1,0:T(8,128)(2,1)}, u32[]{:S(2)}, u32[]{:S(2)}) collective-permute-start(bf16[4,4,128,256]{3,2,1,0:T(8,128)(2,1)} %broadcast_select_fusion), channel_id=1, source_target_pairs={{0,4},{4,0},{1,5},{5,1},{2,6},{6,2},{3,7},{7,3},{8,12},{12,8},{9,1... | collective-permute-start | bytes 3145736 | tf_op jit(solution)/shard_map/ppermute | solution.py:257
  82.3 8.2 %collective-permute-start.4 = (bf16[4,4,128,256]{3,2,1,0:T(8,128)(2,1)}, bf16[4,4,128,256]{3,2,1,0:T(8,128)(2,1)}, u32[]{:S(2)}, u32[]{:S(2)}) collective-permute-start(bf16[4,4,128,256]{3,2,1,0:T(8,128)(2,1)} %maximum_select_fusion), channel_id=1, source_target_pairs={{0,4},{4,0},{1,5},{5,1},{2,6},{6,2},{3,7},{7,3},{8,12},{12,8},{9,1... | collective-permute-start | bytes 3145736 | tf_op jit(solution)/shard_map/ppermute | solution.py:257
  109.1 47.6 %all-to-all-start.4 = ((bf16[128,16,512]{2,1,0:T(8,128)(2,1)}), bf16[128,16,512]{2,1,0:T(8,128)(2,1)}, u32[]{:S(2)}, u32[]{:S(2)}) async-start(bf16[128,16,512]{2,1,0:T(8,128)(2,1)} %bitcast.15), calls=%async_computation.4 | async-start | bytes 4194304 | tf_op jit(solution)/shard_map/all_to_all | solution.py:284

commit v5 on v4

--- a/solution.py
+++ b/solution.py
@@ -174,10 +174,13 @@
                 pltpu.SMEM((32,), jnp.int32),
             ],
         ),
-        compiler_params=pltpu.CompilerParams(vmem_limit_bytes=48 << 20),
+        compiler_params=pltpu.CompilerParams(vmem_limit_bytes=VM << 20),
         cost_estimate=pl.CostEstimate(flops=work, bytes_accessed=16 << 20, transcendentals=0),
         name="attend",
     )(docs, plan, at, q, *kv)
+
+
+VM = 52
 
 
 AXES = ("y", "z", "core", "x")
@@ -229,24 +232,44 @@
     )(seat, tab, rows)
 
 
-def place_kernel(*refs):
-    out = refs[-1]
-    for first, size, part in zip(FIRST, SIZES, refs[:-1]):
+def place_kernel(first, size, part, *refs):
+    out, buf, sem = refs[-3:]
+    step = pl.program_id(0)
+
+    def copy(y, x):
+        cols = pl.ds(pl.multiple_of((y * 4 + x) * 1024 + first * 128, 128), size * 128)
+        return pltpu.make_async_copy(buf.at[y, x], out.at[:, cols], sem.at[y, x])
+
+    for x in range(4):
         for b in range(8):
+            buf[step, x, b * 16:b * 16 + 16, :] = part[0, b, x]
+        copy(step, x).start()
+
+    @pl.when(step == 3)
+    def _():
+        for y in range(4):
             for x in range(4):
-                col = x * 1024 + first * 128
-                out[b * 16:b * 16 + 16, col:col + size * 128] = part[0, b, x]
-
-
-def place(parts):
+                copy(y, x).wait()
+
+
+def place(first, size, part, rows):
+    before = [] if rows is None else [rows]
     return pl.pallas_call(
-        place_kernel,
+        functools.partial(place_kernel, first, size),
         grid=(4,),
         out_shape=jax.ShapeDtypeStruct((128, 16384), jnp.bfloat16),
-        in_specs=[pl.BlockSpec((1, 8, 4, 16, n * 128), lambda y: (y, 0, 0, 0, 0)) for n in SIZES],
-        out_specs=pl.BlockSpec((128, 4096), lambda y: (0, y)),
+        in_specs=[pl.BlockSpec((1, 8, 4, 16, size * 128), lambda y: (y, 0, 0, 0, 0))]
+        + [pl.BlockSpec(memory_space=pl.ANY)] * len(before),
+        out_specs=pl.BlockSpec(memory_space=pl.ANY),
+        scratch_shapes=[
+            pltpu.VMEM((4, 4, 128, size * 128), jnp.bfloat16),
+            pltpu.SemaphoreType.DMA((4, 4)),
+        ],
+        input_output_aliases={1: 0} if before else {},
+        compiler_params=pltpu.CompilerParams(vmem_limit_bytes=12 << 20),
+        cost_estimate=pl.CostEstimate(flops=1 << 30, bytes_accessed=4 << 20, transcendentals=0),
         name="place",
-    )(*parts)
+    )(part, *before)
 
 
 def ring(a, by):
@@ -276,14 +299,14 @@
     third = jnp.where(core == 0, middle, jnp.concatenate([far_keys, far_values], axis=-1))
     third = swap(third)
     kv = (far_keys, far_values, third, near, first, own)
-    done = []
+    rows = None
     for j, (size, part) in enumerate(zip(SIZES, parts)):
         if j > 0:
             part = lax.all_to_all(part, ("y", "x"), split_axis=0, concat_axis=0, tiled=True)
         o = attend(size, doc_lengths, block_plan, at, part.reshape(4, 4, 128, size * 128), kv)
         o = lax.all_to_all(o.reshape(128, 16, size * 128), AXES, split_axis=0, concat_axis=0, tiled=True)
-        done.append(o.reshape(4, 8, 4, 16, size * 128))
-    return place(done)
+        rows = place(FIRST[j], size, o.reshape(4, 8, 4, 16, size * 128), rows)
+    return rows
 
 
 def solution(mesh):

time: 198 us -> 190 us (0.960)
  blocking collectives: 35.6 us -> 0 us
  waiting for transfers between devices: 57.7 us -> 91.3 us
  starting transfers between devices: 50.5 us -> 41.9 us
    all_to_all x1 -> x0, blocking collectives: 35.6 us -> none  [on_device(): lax.all_to_all(o.reshape(128, 16, size * 128), AXES, split_axis=0, concat...]
    all_to_all x1 -> x2, waiting for transfers between devices: 12.2 us -> 41.6 us  [on_device(): lax.all_to_all(o.reshape(128, 16, size * 128), AXES, split_axis=0, concat...]
    all_to_all x1, waiting for transfers between devices: 21.6 us -> 0.01 us  [on_device(): lax.all_to_all(parts[0], ('y', 'x'), split_axis=0, concat_axis=0, tiled=T...]
    ppermute x4, waiting for transfers between devices: 8.75 us -> 25.3 us  [ring(): return lax.ppermute(a, 'z', [(i, (i + by) % 4) for i in range(4)])]
    all_to_all x1, waiting for transfers between devices: 4.82 us -> 14.1 us  [on_device(): lax.all_to_all(part, ('y', 'x'), split_axis=0, concat_axis=0, tiled=True)]
    all_to_all x1 -> x2, starting transfers between devices: 17 us -> 9.65 us  [on_device(): lax.all_to_all(o.reshape(128, 16, size * 128), AXES, split_axis=0, concat...]
    pallas_call x1 -> x2, Pallas kernels: 4.68 us -> 5.08 us  [place(): pl.pallas_call(functools.partial(place_kernel, first, size), grid=(4,), o...]
  transfers between devices with their start and end apart: 10 -> 11, of which waited for: 6 -> 7; matrix products, arithmetic and copies ran while one was open for 2% -> 2% of each run, Pallas kernels for 12% -> 24%
where the time goes in v5:
time: 190 us; the launch traced here: 189 us
  waiting for transfers between devices  91.3 us (48%)
  Pallas kernels  50.6 us (27%)
  starting transfers between devices  41.9 us (22%)
  local copies, waits for them, and re-layouts  2.4 us (1%)
  other arithmetic  2.39 us (1%)
    all_to_all x2, waiting for transfers between devices, on_device(): lax.all_to_all(o.reshape(128, 16, size * 128), AXES, split_axis=0, concat...  41.6 us
    pallas_call x2, Pallas kernels, attend(): pl.pallas_call(lambda *r: attn_kernel(heads, *r), out_shape=jax.ShapeDtyp...  37.5 us
    ppermute x4, waiting for transfers between devices, ring(): return lax.ppermute(a, 'z', [(i, (i + by) % 4) for i in range(4)])  25.3 us
    all_to_all x1, waiting for transfers between devices, on_device(): lax.all_to_all(part, ('y', 'x'), split_axis=0, concat_axis=0, tiled=True)  14.1 us
    all_to_all x1, waiting for transfers between devices, on_device(): lax.all_to_all(kv, ('y', 'x'), split_axis=0, concat_axis=0, tiled=True)  10.3 us
    all_to_all x2, starting transfers between devices, on_device(): lax.all_to_all(o.reshape(128, 16, size * 128), AXES, split_axis=0, concat...  9.65 us
    all_to_all x1, starting transfers between devices, on_device(): lax.all_to_all(kv, ('y', 'x'), split_axis=0, concat_axis=0, tiled=True)  7.57 us
    ppermute x4, starting transfers between devices, ring(): return lax.ppermute(a, 'z', [(i, (i + by) % 4) for i in range(4)])  7.18 us
  transfers between devices with their start and end apart: 11, of which 7 were waited for; matrix products, arithmetic and copies ran while one was open for 2% of the time, Pallas kernels for 24%

profile of v5, /device:TPU:1, one launch (start us, length us, event | category | flops | bytes accessed | tf_op | source)
XLA Modules:
  0.0 188.9 jit_solution(9585894571594036830)
XLA Ops:
  0.0 2.3 %pack.1 = bf16[16,128,256]{2,1,0:T(8,128)(2,1)} custom-call(s32[1]{0:T(128)} %bitcast.1.seat, f32[512,128]{1,0:T(8,128)} %constant.26.clone.tab, bf16[128,1024]{1,0:T(8,128)(2,1)} %keys.1, bf16[128,1024]{1,0:T(8,128)(2,1)} %values.1), custom_call_target="tpu_custom_call" | custom-call | tf_op jit(solution)/shard_map/pack/pallas_call | solution.py:202
  2.3 7.6 %all-to-all-start = ((bf16[16,128,256]{2,1,0:T(8,128)(2,1)}), bf16[16,128,256]{2,1,0:T(8,128)(2,1)S(1)}, u32[]{:S(2)}, u32[]{:S(2)}) async-start(bf16[16,128,256]{2,1,0:T(8,128)(2,1)} %pack.1), calls=%async_computation | async-start | bytes 2097152 | tf_op jit(solution)/shard_map/all_to_all | solution.py:289
  9.9 5.7 %split.1 = (bf16[16,128,512]{2,1,0:T(8,128)(2,1)}, bf16[16,128,512]{2,1,0:T(8,128)(2,1)}) custom-call(s32[1]{0:T(128)} %bitcast.1.seat, f32[512,128]{1,0:T(8,128)} %constant.26.clone.tab, bf16[128,16384]{1,0:T(8,128)(2,1)} %rows.1), custom_call_target="tpu_custom_call" | custom-call | flops 2147483648 | bytes 8388608 | tf_op jit(solution)/shard_map/split/pallas_call | solution.py:220
  15.6 10.3 %all-to-all-done = bf16[16,128,256]{2,1,0:T(8,128)(2,1)S(1)} async-done(((bf16[16,128,256]{2,1,0:T(8,128)(2,1)}), bf16[16,128,256]{2,1,0:T(8,128)(2,1)S(1)}, u32[]{:S(2)}, u32[]{:S(2)}) %all-to-all-start) | async-done | bytes 1048608 | tf_op jit(solution)/shard_map/all_to_all | solution.py:289
  25.9 4.4 %all-to-all-start.2 = ((bf16[16,128,512]{2,1,0:T(8,128)(2,1)}), bf16[16,128,512]{2,1,0:T(8,128)(2,1)}, u32[]{:S(2)}, u32[]{:S(2)}) async-start(bf16[16,128,512]{2,1,0:T(8,128)(2,1)} %get-tuple-element.16), calls=%async_computation.2 | async-start | bytes 4194304 | tf_op jit(solution)/shard_map/all_to_all | solution.py:297
  30.4 1.7 collective-permute-start
  32.2 2.2 %collective-permute-start.2 = (bf16[4,4,128,128]{3,2,1,0:T(8,128)(2,1)S(1)}, bf16[4,4,128,128]{3,2,1,0:T(8,128)(2,1)}, u32[]{:S(2)}, u32[]{:S(2)}) collective-permute-start(bf16[4,4,128,128]{3,2,1,0:T(8,128)(2,1)S(1)} %slice.7), channel_id=1, source_target_pairs={{0,24},{8,0},{16,8},{24,16},{1,25},{9,1},{17,9},{25,17},{2,26},{10... | collective-permute-start | bytes 1572872 | tf_op jit(solution)/shard_map/ppermute | solution.py:276
  34.4 8.9 %collective-permute-done.2 = bf16[4,4,128,128]{3,2,1,0:T(8,128)(2,1)} collective-permute-done((bf16[4,4,128,128]{3,2,1,0:T(8,128)(2,1)S(1)}, bf16[4,4,128,128]{3,2,1,0:T(8,128)(2,1)}, u32[]{:S(2)}, u32[]{:S(2)}) %collective-permute-start.2) | collective-permute-done | bytes 524320 | tf_op jit(solution)/shard_map/ppermute | solution.py:276
  43.3 3.3 %collective-permute-start.3 = (bf16[4,4,128,128]{3,2,1,0:T(8,128)(2,1)}, bf16[4,4,128,128]{3,2,1,0:T(8,128)(2,1)S(1)}, u32[]{:S(2)}, u32[]{:S(2)}) collective-permute-start(bf16[4,4,128,128]{3,2,1,0:T(8,128)(2,1)} %collective-permute-done.2), channel_id=1, source_target_pairs={{0,24},{8,0},{16,8},{24,16},{1,25},{9,1},{17,9},{25,17},{2,26},{10... | collective-permute-start | bytes 1572872 | tf_op jit(solution)/shard_map/ppermute | solution.py:276
  46.6 8.7 %collective-permute-done.r_7_ = bf16[4,4,128,256]{3,2,1,0:T(8,128)(2,1)S(1)} collective-permute-done((bf16[4,4,128,256]{3,2,1,0:T(8,128)(2,1)S(1)}, bf16[4,4,128,256]{3,2,1,0:T(8,128)(2,1)S(1)}, u32[]{:S(2)}, u32[]{:S(2)}) %collective-permute-start) | collective-permute-done | bytes 1048608 | tf_op jit(solution)/shard_map/ppermute | solution.py:276
  57.3 3.1 %collective-permute-start.5 = (bf16[4,4,128,256]{3,2,1,0:T(8,128)(2,1)}, bf16[4,4,128,256]{3,2,1,0:T(8,128)(2,1)}, u32[]{:S(2)}, u32[]{:S(2)}) collective-permute-start(bf16[4,4,128,256]{3,2,1,0:T(8,128)(2,1)} %broadcast_select_fusion), channel_id=1, source_target_pairs={{0,4},{4,0},{1,5},{5,1},{2,6},{6,2},{3,7},{7,3},{8,12},{12,8},{9,1... | collective-permute-start | bytes 3145736 | tf_op jit(solution)/shard_map/ppermute | solution.py:280
  60.4 7.7 %collective-permute-done.1.r_4_ = bf16[4,4,128,128]{3,2,1,0:T(8,128)(2,1)S(1)} collective-permute-done((bf16[4,4,128,128]{3,2,1,0:T(8,128)(2,1)}, bf16[4,4,128,128]{3,2,1,0:T(8,128)(2,1)S(1)}, u32[]{:S(2)}, u32[]{:S(2)}) %collective-permute-start.1) | collective-permute-done | bytes 524320 | tf_op jit(solution)/shard_map/ppermute | solution.py:276
  69.4 3.9 %collective-permute-start.4 = (bf16[4,4,128,256]{3,2,1,0:T(8,128)(2,1)}, bf16[4,4,128,256]{3,2,1,0:T(8,128)(2,1)}, u32[]{:S(2)}, u32[]{:S(2)}) collective-permute-start(bf16[4,4,128,256]{3,2,1,0:T(8,128)(2,1)} %maximum_select_fusion), channel_id=1, source_target_pairs={{0,4},{4,0},{1,5},{5,1},{2,6},{6,2},{3,7},{7,3},{8,12},{12,8},{9,1... | collective-permute-start | bytes 3145736 | tf_op jit(solution)/shard_map/ppermute | solution.py:280
  73.3 6.1 %all-to-all-start.1 = ((bf16[16,128,512]{2,1,0:T(8,128)(2,1)}), bf16[16,128,512]{2,1,0:T(8,128)(2,1)S(1)}, u32[]{:S(2)}, u32[]{:S(2)}) async-start(bf16[16,128,512]{2,1,0:T(8,128)(2,1)} %get-tuple-element.14), calls=%async_computation.1 | async-start | bytes 4194304 | tf_op jit(solution)/shard_map/all_to_all | solution.py:305
  79.4 18.8 %attend.3 = bf16[32,4,16,512]{3,2,1,0:T(8,128)(2,1)} custom-call(s32[16]{0:T(128)S(1)} %copy-done.1, s32[32,32]{1,0:T(8,128)S(1)} %copy-done, s32[1]{0:T(128)} %bitcast.r_2_, bf16[4,4,128,512]{3,2,1,0:T(8,128)(2,1)} %bitcast.6.r_3_, bf16[4,4,128,128]{3,2,1,0:T(8,128)(2,1)S(1)} %collective-permute-done.1.r_4_, ...), custom_call_target="tpu_custom_call" | custom-call | flops 19327352832 | bytes 16777216 | tf_op jit(solution)/shard_map/attend/pallas_call | solution.py:160
  98.2 14.1 %all-to-all-done.1 = bf16[16,128,512]{2,1,0:T(8,128)(2,1)S(1)} async-done(((bf16[16,128,512]{2,1,0:T(8,128)(2,1)}), bf16[16,128,512]{2,1,0:T(8,128)(2,1)S(1)}, u32[]{:S(2)}, u32[]{:S(2)}) %all-to-all-start.1) | async-done | bytes 2097184 | tf_op jit(solution)/shard_map/all_to_all | solution.py:305
  112.3 1.3 copy-done.4
  113.6 4.9 %all-to-all-start.4 = ((bf16[128,16,512]{2,1,0:T(8,128)(2,1)}), bf16[128,16,512]{2,1,0:T(8,128)(2,1)S(1)}, u32[]{:S(2)}, u32[]{:S(2)}) async-start(bf16[128,16,512]{2,1,0:T(8,128)(2,1)} %bitcast.16), calls=%async_computation.4 | async-start | bytes 4194304 | tf_op jit(solution)/shard_map/all_to_all | solution.py:307
  118.6 18.7 %attend.2 = bf16[32,4,16,512]{3,2,1,0:T(8,128)(2,1)} custom-call(s32[16]{0:T(128)S(1)} %copy-done.1, s32[32,32]{1,0:T(8,128)S(1)} %copy-done, s32[1]{0:T(128)} %bitcast.r_2_, bf16[4,4,128,512]{3,2,1,0:T(8,128)(2,1)} %bitcast.15, bf16[4,4,128,128]{3,2,1,0:T(8,128)(2,1)S(1)} %collective-permute-done.1.r_4_, ...), custom_call_target="tpu_custom_call" | custom-call | flops 19327352832 | bytes 16777216 | tf_op jit(solution)/shard_map/attend/pallas_call | solution.py:160
  137.3 12.4 %all-to-all-done.4 = bf16[128,16,512]{2,1,0:T(8,128)(2,1)S(1)} async-done(((bf16[128,16,512]{2,1,0:T(8,128)(2,1)}), bf16[128,16,512]{2,1,0:T(8,128)(2,1)S(1)}, u32[]{:S(2)}, u32[]{:S(2)}) %all-to-all-start.4) | async-done | bytes 2097184 | tf_op jit(solution)/shard_map/all_to_all | solution.py:307
  149.7 4.7 %all-to-all-start.3 = ((bf16[128,16,512]{2,1,0:T(8,128)(2,1)}), bf16[128,16,512]{2,1,0:T(8,128)(2,1)}, u32[]{:S(2)}, u32[]{:S(2)}) async-start(bf16[128,16,512]{2,1,0:T(8,128)(2,1)} %bitcast.17), calls=%async_computation.3 | async-start | bytes 4194304 | tf_op jit(solution)/shard_map/all_to_all | solution.py:307
  154.4 1.5 place.2.refs_0_
  155.9 29.2 %all-to-all-done.3 = bf16[128,16,512]{2,1,0:T(8,128)(2,1)} async-done(((bf16[128,16,512]{2,1,0:T(8,128)(2,1)}), bf16[128,16,512]{2,1,0:T(8,128)(2,1)}, u32[]{:S(2)}, u32[]{:S(2)}) %all-to-all-start.3) | async-done | bytes 2097184 | tf_op jit(solution)/shard_map/all_to_all | solution.py:307
  185.1 3.6 %place.3 = bf16[128,16384]{1,0:T(8,128)(2,1)} custom-call(bf16[4,8,4,16,512]{4,3,2,1,0:T(8,128)(2,1)} %bitcast.5.part, bf16[128,16384]{1,0:T(8,128)(2,1)} %place.2.refs_0_), custom_call_target="tpu_custom_call", output_to_operand_aliasing={{}: (1, {})} | custom-call | flops 1073741824 | bytes 4194304 | tf_op jit(solution)/shard_map/place/pallas_call | solution.py:257
  (18 shorter events, 3.5 us)
Async XLA Ops:
  2.3 23.6 %all-to-all-start = ((bf16[16,128,256]{2,1,0:T(8,128)(2,1)}), bf16[16,128,256]{2,1,0:T(8,128)(2,1)S(1)}, u32[]{:S(2)}, u32[]{:S(2)}) async-start(bf16[16,128,256]{2,1,0:T(8,128)(2,1)} %pack.1), calls=%async_computation | async-start | bytes 2097152 | tf_op jit(solution)/shard_map/all_to_all | solution.py:289
  25.9 30.3 %copy-start.2 = (bf16[16,128,256]{2,1,0:T(8,128)(2,1)}, bf16[16,128,256]{2,1,0:T(8,128)(2,1)S(1)}, u32[]{:S(2)}) copy-start(bf16[16,128,256]{2,1,0:T(8,128)(2,1)S(1)} %all-to-all-done) | copy-start | bytes 3145732
  25.9 34.5 %all-to-all-start.2 = ((bf16[16,128,512]{2,1,0:T(8,128)(2,1)}), bf16[16,128,512]{2,1,0:T(8,128)(2,1)}, u32[]{:S(2)}, u32[]{:S(2)}) async-start(bf16[16,128,512]{2,1,0:T(8,128)(2,1)} %get-tuple-element.16), calls=%async_computation.2 | async-start | bytes 4194304 | tf_op jit(solution)/shard_map/all_to_all | solution.py:297
  30.4 24.9 %collective-permute-start = (bf16[4,4,128,256]{3,2,1,0:T(8,128)(2,1)S(1)}, bf16[4,4,128,256]{3,2,1,0:T(8,128)(2,1)S(1)}, u32[]{:S(2)}, u32[]{:S(2)}) collective-permute-start(bf16[4,4,128,256]{3,2,1,0:T(8,128)(2,1)S(1)} %bitcast.10), channel_id=1, source_target_pairs={{0,8},{8,16},{16,24},{24,0},{1,9},{9,17},{17,25},{25,1},{2,10},{10... | collective-permute-start | bytes 3145736 | tf_op jit(solution)/shard_map/ppermute | solution.py:276
  32.2 11.1 %collective-permute-start.2 = (bf16[4,4,128,128]{3,2,1,0:T(8,128)(2,1)S(1)}, bf16[4,4,128,128]{3,2,1,0:T(8,128)(2,1)}, u32[]{:S(2)}, u32[]{:S(2)}) collective-permute-start(bf16[4,4,128,128]{3,2,1,0:T(8,128)(2,1)S(1)} %slice.7), channel_id=1, source_target_pairs={{0,24},{8,0},{16,8},{24,16},{1,25},{9,1},{17,9},{25,17},{2,26},{10... | collective-permute-start | bytes 1572872 | tf_op jit(solution)/shard_map/ppermute | solution.py:276
  43.3 17.1 %collective-permute-start.3 = (bf16[4,4,128,128]{3,2,1,0:T(8,128)(2,1)}, bf16[4,4,128,128]{3,2,1,0:T(8,128)(2,1)S(1)}, u32[]{:S(2)}, u32[]{:S(2)}) collective-permute-start(bf16[4,4,128,128]{3,2,1,0:T(8,128)(2,1)} %collective-permute-done.2), channel_id=1, source_target_pairs={{0,24},{8,0},{16,8},{24,16},{1,25},{9,1},{17,9},{25,17},{2,26},{10... | collective-permute-start | bytes 1572872 | tf_op jit(solution)/shard_map/ppermute | solution.py:276
  55.3 12.8 %copy-start.3 = (bf16[4,4,128,256]{3,2,1,0:T(8,128)(2,1)}, bf16[4,4,128,256]{3,2,1,0:T(8,128)(2,1)S(1)}, u32[]{:S(2)}) copy-start(bf16[4,4,128,256]{3,2,1,0:T(8,128)(2,1)S(1)} %collective-permute-done.r_7_) | copy-start | bytes 3145732
  56.2 11.8 %collective-permute-start.1 = (bf16[4,4,128,128]{3,2,1,0:T(8,128)(2,1)}, bf16[4,4,128,128]{3,2,1,0:T(8,128)(2,1)S(1)}, u32[]{:S(2)}, u32[]{:S(2)}) collective-permute-start(bf16[4,4,128,128]{3,2,1,0:T(8,128)(2,1)} %slice.8), channel_id=1, source_target_pairs={{0,8},{8,16},{16,24},{24,0},{1,9},{9,17},{17,25},{25,1},{2,10},{10... | collective-permute-start | bytes 1572872 | tf_op jit(solution)/shard_map/ppermute | solution.py:276
  57.3 22.1 %collective-permute-start.5 = (bf16[4,4,128,256]{3,2,1,0:T(8,128)(2,1)}, bf16[4,4,128,256]{3,2,1,0:T(8,128)(2,1)}, u32[]{:S(2)}, u32[]{:S(2)}) collective-permute-start(bf16[4,4,128,256]{3,2,1,0:T(8,128)(2,1)} %broadcast_select_fusion), channel_id=1, source_target_pairs={{0,4},{4,0},{1,5},{5,1},{2,6},{6,2},{3,7},{7,3},{8,12},{12,8},{9,1... | collective-permute-start | bytes 3145736 | tf_op jit(solution)/shard_map/ppermute | solution.py:280
  69.4 10.0 %copy-start = (s32[32,32]{1,0:T(8,128)S(1)}, s32[32,32]{1,0:T(8,128)}, u32[]{:S(2)}) copy-start(s32[32,32]{1,0:T(8,128)} %r_1_.3) | copy-start | bytes 12292
  69.4 10.0 %copy-start.1 = (s32[16]{0:T(128)S(1)}, s32[16]{0:T(128)}, u32[]{:S(2)}) copy-start(s32[16]{0:T(128)} %r_0_.3) | copy-start | bytes 196
  69.4 10.0 %collective-permute-start.4 = (bf16[4,4,128,256]{3,2,1,0:T(8,128)(2,1)}, bf16[4,4,128,256]{3,2,1,0:T(8,128)(2,1)}, u32[]{:S(2)}, u32[]{:S(2)}) collective-permute-start(bf16[4,4,128,256]{3,2,1,0:T(8,128)(2,1)} %maximum_select_fusion), channel_id=1, source_target_pairs={{0,4},{4,0},{1,5},{5,1},{2,6},{6,2},{3,7},{7,3},{8,12},{12,8},{9,1... | collective-permute-start | bytes 3145736 | tf_op jit(solution)/shard_map/ppermute | solution.py:280
  73.3 39.0 %all-to-all-start.1 = ((bf16[16,128,512]{2,1,0:T(8,128)(2,1)}), bf16[16,128,512]{2,1,0:T(8,128)(2,1)S(1)}, u32[]{:S(2)}, u32[]{:S(2)}) async-start(bf16[16,128,512]{2,1,0:T(8,128)(2,1)} %get-tuple-element.14), calls=%async_computation.1 | async-start | bytes 4194304 | tf_op jit(solution)/shard_map/all_to_all | solution.py:305
  112.3 1.3 copy-start.4
  113.6 36.0 %all-to-all-start.4 = ((bf16[128,16,512]{2,1,0:T(8,128)(2,1)}), bf16[128,16,512]{2,1,0:T(8,128)(2,1)S(1)}, u32[]{:S(2)}, u32[]{:S(2)}) async-start(bf16[128,16,512]{2,1,0:T(8,128)(2,1)} %bitcast.16), calls=%async_computation.4 | async-start | bytes 4194304 | tf_op jit(solution)/shard_map/all_to_all | solution.py:307
  149.7 35.4 %all-to-all-start.3 = ((bf16[128,16,512]{2,1,0:T(8,128)(2,1)}), bf16[128,16,512]{2,1,0:T(8,128)(2,1)}, u32[]{:S(2)}, u32[]{:S(2)}) async-start(bf16[128,16,512]{2,1,0:T(8,128)(2,1)} %bitcast.17), calls=%async_computation.3 | async-start | bytes 4194304 | tf_op jit(solution)/shard_map/all_to_all | solution.py:307

commit v6 on v5

--- a/solution.py
+++ b/solution.py
@@ -250,6 +250,42 @@
         for y in range(4):
             for x in range(4):
                 copy(y, x).wait()
+
+
+def place_last_kernel(first, size, part, rows, out, land, buf, got, sem):
+    fetches = [pltpu.make_async_copy(part.at[y], land.at[y], got.at[y]) for y in range(4)]
+    for fetch in fetches:
+        fetch.start()
+    copies = []
+    for y in range(4):
+        fetches[y].wait()
+        for x in range(4):
+            for b in range(8):
+                buf[y, x, b * 16:b * 16 + 16, :] = land[y, b, x]
+            cols = pl.ds((y * 4 + x) * 1024 + first * 128, size * 128)
+            copies.append(pltpu.make_async_copy(buf.at[y, x], out.at[:, cols], sem.at[y, x]))
+            copies[-1].start()
+    for c in copies:
+        c.wait()
+
+
+def place_last(first, size, part, rows):
+    return pl.pallas_call(
+        functools.partial(place_last_kernel, first, size),
+        out_shape=jax.ShapeDtypeStruct((128, 16384), jnp.bfloat16),
+        in_specs=[pl.BlockSpec(memory_space=pltpu.HBM), pl.BlockSpec(memory_space=pl.ANY)],
+        out_specs=pl.BlockSpec(memory_space=pl.ANY),
+        scratch_shapes=[
+            pltpu.VMEM((4, 8, 4, 16, size * 128), jnp.bfloat16),
+            pltpu.VMEM((4, 4, 128, size * 128), jnp.bfloat16),
+            pltpu.SemaphoreType.DMA((4,)),
+            pltpu.SemaphoreType.DMA((4, 4)),
+        ],
+        input_output_aliases={1: 0},
+        compiler_params=pltpu.CompilerParams(vmem_limit_bytes=12 << 20),
+        cost_estimate=pl.CostEstimate(flops=1 << 30, bytes_accessed=4 << 20, transcendentals=0),
+        name="place",
+    )(part, rows)
 
 
 def place(first, size, part, rows):
@@ -305,7 +341,8 @@
             part = lax.all_to_all(part, ("y", "x"), split_axis=0, concat_axis=0, tiled=True)
         o = attend(size, doc_lengths, block_plan, at, part.reshape(4, 4, 128, size * 128), kv)
         o = lax.all_to_all(o.reshape(128, 16, size * 128), AXES, split_axis=0, concat_axis=0, tiled=True)
-        rows = place(FIRST[j], size, o.reshape(4, 8, 4, 16, size * 128), rows)
+        put = place if rows is None else place_last
+        rows = put(FIRST[j], size, o.reshape(4, 8, 4, 16, size * 128), rows)
     return rows
 
 

time: 190 us -> 188 us (0.989)
    pallas_call x2 -> x1, Pallas kernels: 5.08 us -> 1.46 us  [place(): pl.pallas_call(functools.partial(place_kernel, first, size), grid=(4,), o...]
    pallas_call x0 -> x1, Pallas kernels: none -> 2.52 us  [place_last(): pl.pallas_call(functools.partial(place_last_kernel, first, size), out_sha...]
where the time goes in v6:
time: 188 us
  waiting for transfers between devices  91.3 us (49%)
  Pallas kernels  49.5 us (26%)
  starting transfers between devices  41.9 us (22%)
  local copies, waits for them, and re-layouts  2.4 us (1%)
  other arithmetic  2.39 us (1%)
    all_to_all x2, waiting for transfers between devices, on_device(): lax.all_to_all(o.reshape(128, 16, size * 128), AXES, split_axis=0, concat...  41.6 us
    pallas_call x2, Pallas kernels, attend(): pl.pallas_call(lambda *r: attn_kernel(heads, *r), out_shape=jax.ShapeDtyp...  37.5 us
    ppermute x4, waiting for transfers between devices, ring(): return lax.ppermute(a, 'z', [(i, (i + by) % 4) for i in range(4)])  25.3 us
    all_to_all x1, waiting for transfers between devices, on_device(): lax.all_to_all(part, ('y', 'x'), split_axis=0, concat_axis=0, tiled=True)  14.1 us
    all_to_all x1, waiting for transfers between devices, on_device(): lax.all_to_all(kv, ('y', 'x'), split_axis=0, concat_axis=0, tiled=True)  10.3 us
    all_to_all x2, starting transfers between devices, on_device(): lax.all_to_all(o.reshape(128, 16, size * 128), AXES, split_axis=0, concat...  9.65 us
    all_to_all x1, starting transfers between devices, on_device(): lax.all_to_all(kv, ('y', 'x'), split_axis=0, concat_axis=0, tiled=True)  7.57 us
    ppermute x4, starting transfers between devices, ring(): return lax.ppermute(a, 'z', [(i, (i + by) % 4) for i in range(4)])  7.18 us
  transfers between devices with their start and end apart: 11, of which 7 were waited for; matrix products, arithmetic and copies ran while one was open for 2% of the time, Pallas kernels for 24%

profile of v6, /device:TPU:1, one launch (start us, length us, event | category | flops | bytes accessed | tf_op | source)
XLA Modules:
  0.0 187.8 jit_solution(3411229691979249330)
XLA Ops:
  0.0 2.3 %pack.1 = bf16[16,128,256]{2,1,0:T(8,128)(2,1)} custom-call(s32[1]{0:T(128)} %bitcast.1.seat, f32[512,128]{1,0:T(8,128)} %constant.26.clone.tab, bf16[128,1024]{1,0:T(8,128)(2,1)} %keys.1, bf16[128,1024]{1,0:T(8,128)(2,1)} %values.1), custom_call_target="tpu_custom_call" | custom-call | tf_op jit(solution)/shard_map/pack/pallas_call | solution.py:202
  2.3 7.6 %all-to-all-start = ((bf16[16,128,256]{2,1,0:T(8,128)(2,1)}), bf16[16,128,256]{2,1,0:T(8,128)(2,1)S(1)}, u32[]{:S(2)}, u32[]{:S(2)}) async-start(bf16[16,128,256]{2,1,0:T(8,128)(2,1)} %pack.1), calls=%async_computation | async-start | bytes 2097152 | tf_op jit(solution)/shard_map/all_to_all | solution.py:325
  9.9 5.7 %split.1 = (bf16[16,128,512]{2,1,0:T(8,128)(2,1)}, bf16[16,128,512]{2,1,0:T(8,128)(2,1)}) custom-call(s32[1]{0:T(128)} %bitcast.1.seat, f32[512,128]{1,0:T(8,128)} %constant.26.clone.tab, bf16[128,16384]{1,0:T(8,128)(2,1)} %rows.1), custom_call_target="tpu_custom_call" | custom-call | flops 2147483648 | bytes 8388608 | tf_op jit(solution)/shard_map/split/pallas_call | solution.py:220
  15.6 10.3 %all-to-all-done = bf16[16,128,256]{2,1,0:T(8,128)(2,1)S(1)} async-done(((bf16[16,128,256]{2,1,0:T(8,128)(2,1)}), bf16[16,128,256]{2,1,0:T(8,128)(2,1)S(1)}, u32[]{:S(2)}, u32[]{:S(2)}) %all-to-all-start) | async-done | bytes 1048608 | tf_op jit(solution)/shard_map/all_to_all | solution.py:325
  25.9 4.4 %all-to-all-start.2 = ((bf16[16,128,512]{2,1,0:T(8,128)(2,1)}), bf16[16,128,512]{2,1,0:T(8,128)(2,1)}, u32[]{:S(2)}, u32[]{:S(2)}) async-start(bf16[16,128,512]{2,1,0:T(8,128)(2,1)} %get-tuple-element.16), calls=%async_computation.2 | async-start | bytes 4194304 | tf_op jit(solution)/shard_map/all_to_all | solution.py:333
  30.4 1.7 collective-permute-start
  32.2 2.2 %collective-permute-start.2 = (bf16[4,4,128,128]{3,2,1,0:T(8,128)(2,1)S(1)}, bf16[4,4,128,128]{3,2,1,0:T(8,128)(2,1)}, u32[]{:S(2)}, u32[]{:S(2)}) collective-permute-start(bf16[4,4,128,128]{3,2,1,0:T(8,128)(2,1)S(1)} %slice.7), channel_id=1, source_target_pairs={{0,24},{8,0},{16,8},{24,16},{1,25},{9,1},{17,9},{25,17},{2,26},{10... | collective-permute-start | bytes 1572872 | tf_op jit(solution)/shard_map/ppermute | solution.py:312
  34.4 8.9 %collective-permute-done.2 = bf16[4,4,128,128]{3,2,1,0:T(8,128)(2,1)} collective-permute-done((bf16[4,4,128,128]{3,2,1,0:T(8,128)(2,1)S(1)}, bf16[4,4,128,128]{3,2,1,0:T(8,128)(2,1)}, u32[]{:S(2)}, u32[]{:S(2)}) %collective-permute-start.2) | collective-permute-done | bytes 524320 | tf_op jit(solution)/shard_map/ppermute | solution.py:312
  43.3 3.3 %collective-permute-start.3 = (bf16[4,4,128,128]{3,2,1,0:T(8,128)(2,1)}, bf16[4,4,128,128]{3,2,1,0:T(8,128)(2,1)S(1)}, u32[]{:S(2)}, u32[]{:S(2)}) collective-permute-start(bf16[4,4,128,128]{3,2,1,0:T(8,128)(2,1)} %collective-permute-done.2), channel_id=1, source_target_pairs={{0,24},{8,0},{16,8},{24,16},{1,25},{9,1},{17,9},{25,17},{2,26},{10... | collective-permute-start | bytes 1572872 | tf_op jit(solution)/shard_map/ppermute | solution.py:312
  46.6 8.7 %collective-permute-done.r_7_ = bf16[4,4,128,256]{3,2,1,0:T(8,128)(2,1)S(1)} collective-permute-done((bf16[4,4,128,256]{3,2,1,0:T(8,128)(2,1)S(1)}, bf16[4,4,128,256]{3,2,1,0:T(8,128)(2,1)S(1)}, u32[]{:S(2)}, u32[]{:S(2)}) %collective-permute-start) | collective-permute-done | bytes 1048608 | tf_op jit(solution)/shard_map/ppermute | solution.py:312
  57.3 3.1 %collective-permute-start.5 = (bf16[4,4,128,256]{3,2,1,0:T(8,128)(2,1)}, bf16[4,4,128,256]{3,2,1,0:T(8,128)(2,1)}, u32[]{:S(2)}, u32[]{:S(2)}) collective-permute-start(bf16[4,4,128,256]{3,2,1,0:T(8,128)(2,1)} %broadcast_select_fusion), channel_id=1, source_target_pairs={{0,4},{4,0},{1,5},{5,1},{2,6},{6,2},{3,7},{7,3},{8,12},{12,8},{9,1... | collective-permute-start | bytes 3145736 | tf_op jit(solution)/shard_map/ppermute | solution.py:316
  60.4 7.7 %collective-permute-done.1.r_4_ = bf16[4,4,128,128]{3,2,1,0:T(8,128)(2,1)S(1)} collective-permute-done((bf16[4,4,128,128]{3,2,1,0:T(8,128)(2,1)}, bf16[4,4,128,128]{3,2,1,0:T(8,128)(2,1)S(1)}, u32[]{:S(2)}, u32[]{:S(2)}) %collective-permute-start.1) | collective-permute-done | bytes 524320 | tf_op jit(solution)/shard_map/ppermute | solution.py:312
  69.4 3.9 %collective-permute-start.4 = (bf16[4,4,128,256]{3,2,1,0:T(8,128)(2,1)}, bf16[4,4,128,256]{3,2,1,0:T(8,128)(2,1)}, u32[]{:S(2)}, u32[]{:S(2)}) collective-permute-start(bf16[4,4,128,256]{3,2,1,0:T(8,128)(2,1)} %maximum_select_fusion), channel_id=1, source_target_pairs={{0,4},{4,0},{1,5},{5,1},{2,6},{6,2},{3,7},{7,3},{8,12},{12,8},{9,1... | collective-permute-start | bytes 3145736 | tf_op jit(solution)/shard_map/ppermute | solution.py:316
  73.3 6.1 %all-to-all-start.1 = ((bf16[16,128,512]{2,1,0:T(8,128)(2,1)}), bf16[16,128,512]{2,1,0:T(8,128)(2,1)S(1)}, u32[]{:S(2)}, u32[]{:S(2)}) async-start(bf16[16,128,512]{2,1,0:T(8,128)(2,1)} %get-tuple-element.14), calls=%async_computation.1 | async-start | bytes 4194304 | tf_op jit(solution)/shard_map/all_to_all | solution.py:341
  79.4 18.8 %attend.3 = bf16[32,4,16,512]{3,2,1,0:T(8,128)(2,1)} custom-call(s32[16]{0:T(128)S(1)} %copy-done.1, s32[32,32]{1,0:T(8,128)S(1)} %copy-done, s32[1]{0:T(128)} %bitcast.r_2_, bf16[4,4,128,512]{3,2,1,0:T(8,128)(2,1)} %bitcast.6.r_3_, bf16[4,4,128,128]{3,2,1,0:T(8,128)(2,1)S(1)} %collective-permute-done.1.r_4_, ...), custom_call_target="tpu_custom_call" | custom-call | flops 19327352832 | bytes 16777216 | tf_op jit(solution)/shard_map/attend/pallas_call | solution.py:160
  98.2 14.1 %all-to-all-done.1 = bf16[16,128,512]{2,1,0:T(8,128)(2,1)S(1)} async-done(((bf16[16,128,512]{2,1,0:T(8,128)(2,1)}), bf16[16,128,512]{2,1,0:T(8,128)(2,1)S(1)}, u32[]{:S(2)}, u32[]{:S(2)}) %all-to-all-start.1) | async-done | bytes 2097184 | tf_op jit(solution)/shard_map/all_to_all | solution.py:341
  112.3 1.3 copy-done.4
  113.6 4.9 %all-to-all-start.4 = ((bf16[128,16,512]{2,1,0:T(8,128)(2,1)}), bf16[128,16,512]{2,1,0:T(8,128)(2,1)S(1)}, u32[]{:S(2)}, u32[]{:S(2)}) async-start(bf16[128,16,512]{2,1,0:T(8,128)(2,1)} %bitcast.16), calls=%async_computation.4 | async-start | bytes 4194304 | tf_op jit(solution)/shard_map/all_to_all | solution.py:343
  118.6 18.7 %attend.2 = bf16[32,4,16,512]{3,2,1,0:T(8,128)(2,1)} custom-call(s32[16]{0:T(128)S(1)} %copy-done.1, s32[32,32]{1,0:T(8,128)S(1)} %copy-done, s32[1]{0:T(128)} %bitcast.r_2_, bf16[4,4,128,512]{3,2,1,0:T(8,128)(2,1)} %bitcast.15, bf16[4,4,128,128]{3,2,1,0:T(8,128)(2,1)S(1)} %collective-permute-done.1.r_4_, ...), custom_call_target="tpu_custom_call" | custom-call | flops 19327352832 | bytes 16777216 | tf_op jit(solution)/shard_map/attend/pallas_call | solution.py:160
  137.3 12.4 %all-to-all-done.4 = bf16[128,16,512]{2,1,0:T(8,128)(2,1)S(1)} async-done(((bf16[128,16,512]{2,1,0:T(8,128)(2,1)}), bf16[128,16,512]{2,1,0:T(8,128)(2,1)S(1)}, u32[]{:S(2)}, u32[]{:S(2)}) %all-to-all-start.4) | async-done | bytes 2097184 | tf_op jit(solution)/shard_map/all_to_all | solution.py:343
  149.7 4.7 %all-to-all-start.3 = ((bf16[128,16,512]{2,1,0:T(8,128)(2,1)}), bf16[128,16,512]{2,1,0:T(8,128)(2,1)}, u32[]{:S(2)}, u32[]{:S(2)}) async-start(bf16[128,16,512]{2,1,0:T(8,128)(2,1)} %bitcast.17), calls=%async_computation.3 | async-start | bytes 4194304 | tf_op jit(solution)/shard_map/all_to_all | solution.py:343
  154.4 1.5 place.2.rows
  155.9 29.2 %all-to-all-done.3 = bf16[128,16,512]{2,1,0:T(8,128)(2,1)} async-done(((bf16[128,16,512]{2,1,0:T(8,128)(2,1)}), bf16[128,16,512]{2,1,0:T(8,128)(2,1)}, u32[]{:S(2)}, u32[]{:S(2)}) %all-to-all-start.3) | async-done | bytes 2097184 | tf_op jit(solution)/shard_map/all_to_all | solution.py:343
  185.1 2.5 %place.3 = bf16[128,16384]{1,0:T(8,128)(2,1)} custom-call(bf16[4,8,4,16,512]{4,3,2,1,0:T(8,128)(2,1)} %bitcast.5.part, bf16[128,16384]{1,0:T(8,128)(2,1)} %place.2.rows), custom_call_target="tpu_custom_call", output_to_operand_aliasing={{}: (1, {})} | custom-call | flops 1073741824 | bytes 4194304 | tf_op jit(solution)/shard_map/place/pallas_call | solution.py:273
  (18 shorter events, 3.5 us)
Async XLA Ops:
  2.3 23.6 %all-to-all-start = ((bf16[16,128,256]{2,1,0:T(8,128)(2,1)}), bf16[16,128,256]{2,1,0:T(8,128)(2,1)S(1)}, u32[]{:S(2)}, u32[]{:S(2)}) async-start(bf16[16,128,256]{2,1,0:T(8,128)(2,1)} %pack.1), calls=%async_computation | async-start | bytes 2097152 | tf_op jit(solution)/shard_map/all_to_all | solution.py:325
  25.9 30.3 %copy-start.2 = (bf16[16,128,256]{2,1,0:T(8,128)(2,1)}, bf16[16,128,256]{2,1,0:T(8,128)(2,1)S(1)}, u32[]{:S(2)}) copy-start(bf16[16,128,256]{2,1,0:T(8,128)(2,1)S(1)} %all-to-all-done) | copy-start | bytes 3145732
  25.9 34.5 %all-to-all-start.2 = ((bf16[16,128,512]{2,1,0:T(8,128)(2,1)}), bf16[16,128,512]{2,1,0:T(8,128)(2,1)}, u32[]{:S(2)}, u32[]{:S(2)}) async-start(bf16[16,128,512]{2,1,0:T(8,128)(2,1)} %get-tuple-element.16), calls=%async_computation.2 | async-start | bytes 4194304 | tf_op jit(solution)/shard_map/all_to_all | solution.py:333
  30.4 24.9 %collective-permute-start = (bf16[4,4,128,256]{3,2,1,0:T(8,128)(2,1)S(1)}, bf16[4,4,128,256]{3,2,1,0:T(8,128)(2,1)S(1)}, u32[]{:S(2)}, u32[]{:S(2)}) collective-permute-start(bf16[4,4,128,256]{3,2,1,0:T(8,128)(2,1)S(1)} %bitcast.10), channel_id=1, source_target_pairs={{0,8},{8,16},{16,24},{24,0},{1,9},{9,17},{17,25},{25,1},{2,10},{10... | collective-permute-start | bytes 3145736 | tf_op jit(solution)/shard_map/ppermute | solution.py:312
  32.2 11.1 %collective-permute-start.2 = (bf16[4,4,128,128]{3,2,1,0:T(8,128)(2,1)S(1)}, bf16[4,4,128,128]{3,2,1,0:T(8,128)(2,1)}, u32[]{:S(2)}, u32[]{:S(2)}) collective-permute-start(bf16[4,4,128,128]{3,2,1,0:T(8,128)(2,1)S(1)} %slice.7), channel_id=1, source_target_pairs={{0,24},{8,0},{16,8},{24,16},{1,25},{9,1},{17,9},{25,17},{2,26},{10... | collective-permute-start | bytes 1572872 | tf_op jit(solution)/shard_map/ppermute | solution.py:312
  43.3 17.1 %collective-permute-start.3 = (bf16[4,4,128,128]{3,2,1,0:T(8,128)(2,1)}, bf16[4,4,128,128]{3,2,1,0:T(8,128)(2,1)S(1)}, u32[]{:S(2)}, u32[]{:S(2)}) collective-permute-start(bf16[4,4,128,128]{3,2,1,0:T(8,128)(2,1)} %collective-permute-done.2), channel_id=1, source_target_pairs={{0,24},{8,0},{16,8},{24,16},{1,25},{9,1},{17,9},{25,17},{2,26},{10... | collective-permute-start | bytes 1572872 | tf_op jit(solution)/shard_map/ppermute | solution.py:312
  55.3 12.8 %copy-start.3 = (bf16[4,4,128,256]{3,2,1,0:T(8,128)(2,1)}, bf16[4,4,128,256]{3,2,1,0:T(8,128)(2,1)S(1)}, u32[]{:S(2)}) copy-start(bf16[4,4,128,256]{3,2,1,0:T(8,128)(2,1)S(1)} %collective-permute-done.r_7_) | copy-start | bytes 3145732
  56.2 11.8 %collective-permute-start.1 = (bf16[4,4,128,128]{3,2,1,0:T(8,128)(2,1)}, bf16[4,4,128,128]{3,2,1,0:T(8,128)(2,1)S(1)}, u32[]{:S(2)}, u32[]{:S(2)}) collective-permute-start(bf16[4,4,128,128]{3,2,1,0:T(8,128)(2,1)} %slice.8), channel_id=1, source_target_pairs={{0,8},{8,16},{16,24},{24,0},{1,9},{9,17},{17,25},{25,1},{2,10},{10... | collective-permute-start | bytes 1572872 | tf_op jit(solution)/shard_map/ppermute | solution.py:312
  57.3 22.1 %collective-permute-start.5 = (bf16[4,4,128,256]{3,2,1,0:T(8,128)(2,1)}, bf16[4,4,128,256]{3,2,1,0:T(8,128)(2,1)}, u32[]{:S(2)}, u32[]{:S(2)}) collective-permute-start(bf16[4,4,128,256]{3,2,1,0:T(8,128)(2,1)} %broadcast_select_fusion), channel_id=1, source_target_pairs={{0,4},{4,0},{1,5},{5,1},{2,6},{6,2},{3,7},{7,3},{8,12},{12,8},{9,1... | collective-permute-start | bytes 3145736 | tf_op jit(solution)/shard_map/ppermute | solution.py:316
  69.4 10.0 %copy-start = (s32[32,32]{1,0:T(8,128)S(1)}, s32[32,32]{1,0:T(8,128)}, u32[]{:S(2)}) copy-start(s32[32,32]{1,0:T(8,128)} %r_1_.3) | copy-start | bytes 12292
  69.4 10.0 %copy-start.1 = (s32[16]{0:T(128)S(1)}, s32[16]{0:T(128)}, u32[]{:S(2)}) copy-start(s32[16]{0:T(128)} %r_0_.3) | copy-start | bytes 196
  69.4 10.0 %collective-permute-start.4 = (bf16[4,4,128,256]{3,2,1,0:T(8,128)(2,1)}, bf16[4,4,128,256]{3,2,1,0:T(8,128)(2,1)}, u32[]{:S(2)}, u32[]{:S(2)}) collective-permute-start(bf16[4,4,128,256]{3,2,1,0:T(8,128)(2,1)} %maximum_select_fusion), channel_id=1, source_target_pairs={{0,4},{4,0},{1,5},{5,1},{2,6},{6,2},{3,7},{7,3},{8,12},{12,8},{9,1... | collective-permute-start | bytes 3145736 | tf_op jit(solution)/shard_map/ppermute | solution.py:316
  73.3 39.0 %all-to-all-start.1 = ((bf16[16,128,512]{2,1,0:T(8,128)(2,1)}), bf16[16,128,512]{2,1,0:T(8,128)(2,1)S(1)}, u32[]{:S(2)}, u32[]{:S(2)}) async-start(bf16[16,128,512]{2,1,0:T(8,128)(2,1)} %get-tuple-element.14), calls=%async_computation.1 | async-start | bytes 4194304 | tf_op jit(solution)/shard_map/all_to_all | solution.py:341
  112.3 1.3 copy-start.4
  113.6 36.0 %all-to-all-start.4 = ((bf16[128,16,512]{2,1,0:T(8,128)(2,1)}), bf16[128,16,512]{2,1,0:T(8,128)(2,1)S(1)}, u32[]{:S(2)}, u32[]{:S(2)}) async-start(bf16[128,16,512]{2,1,0:T(8,128)(2,1)} %bitcast.16), calls=%async_computation.4 | async-start | bytes 4194304 | tf_op jit(solution)/shard_map/all_to_all | solution.py:343
  149.7 35.4 %all-to-all-start.3 = ((bf16[128,16,512]{2,1,0:T(8,128)(2,1)}), bf16[128,16,512]{2,1,0:T(8,128)(2,1)}, u32[]{:S(2)}, u32[]{:S(2)}) async-start(bf16[128,16,512]{2,1,0:T(8,128)(2,1)} %bitcast.17), calls=%async_computation.3 | async-start | bytes 4194304 | tf_op jit(solution)/shard_map/all_to_all | solution.py:343
